TPU v7x, 32 devices: a 4x4x1 block of a 4x4x8 slice. The times are simulated.
32 devices in a mesh: replica: 1 (over z), data: 4 (over y), model: 8 (over x, core).
Axes of the slice: x: 4, y: 4, z: 1, core: 2. Of those that a mesh axis runs over, the one named last changes fastest.
The devices are a block of a 4x4x8 slice.
Arguments:
- x_in: bfloat16 [32768, 1024], P(('replica', 'data'))
- w_in: bfloat16 [1024, 1024], P(('replica', 'model'))
- w_mid: bfloat16 [1024, 1024], P(('replica', 'model'))
- w_out: bfloat16 [1024, 1024], P(('replica', 'model'))
- u_in: float32 [1024], P(('replica', 'model'))
- u_mid: float32 [1024], P(('replica', 'model'))
- u_out: float32 [1024], P(('replica', 'model'))
- target: bfloat16 [32768, 1024], P(('replica', 'data'), 'model')
Outputs:
- output 1: float32 [1], P('replica')
- output 2: bfloat16 [32768, 1024], P(('replica', 'data'))
- output 3: float32 [1024, 1024], P(('replica', 'model'))
- output 4: float32 [1024, 1024], P(('replica', 'model'))
- output 5: float32 [1024, 1024], P(('replica', 'model'))
- output 6: float32 [1024], P(('replica', 'model'))
- output 7: float32 [1024], P(('replica', 'model'))
- output 8: float32 [1024], P(('replica', 'model'))
- output 9: float32 [1024], P('replica')
- output 10: float32 [1024], P('replica')
- output 11: float32 [1024], P('replica')
- output 12: float32 [3], P('replica')
All inputs are finite; a program needn't handle non-finite values.
Results may differ from a plain program's by a relative error of at most 0.02.
Values are sent between devices in bfloat16 or wider.
A program may use at most 768 MiB of HBM per device.

v0:
```python
import jax
import jax.numpy as jnp
from jax import lax
from jax.sharding import PartitionSpec as P

MATVEC_PRECISION = lax.Precision.HIGHEST


def solution(mesh):
    data_size = mesh.shape["data"]
    row_spec = P(("replica", "model"), None)
    vec_spec = P(("replica", "model"))
    batch_spec = P(("replica", "data"), None)
    target_spec = P(("replica", "data"), "model")
    part_spec = P("replica")

    def local_step(x_in, w_in, w_mid, w_out, u_in, u_mid, u_out, target):
        batch_total = x_in.shape[0] * data_size
        weights = [w_in, w_mid, w_out]
        u_vecs = [u_in, u_mid, u_out]
        saved_in = []
        saved_out = []
        layer_stats = []
        for layer_idx in range(3):
            weight = weights[layer_idx]
            partial_p = jnp.dot(u_vecs[layer_idx], weight, preferred_element_type=jnp.float32, precision=MATVEC_PRECISION)
            p_vec = lax.psum(partial_p, "model")
            v_vec = p_vec / jnp.maximum(jnp.sqrt(jnp.sum(p_vec * p_vec)), 1e-12)
            s_vec = jnp.dot(weight, v_vec, preferred_element_type=jnp.float32, precision=MATVEC_PRECISION)
            sigma_val = jnp.sqrt(lax.psum(jnp.sum(s_vec * s_vec), "model"))
            if layer_idx == 0:
                layer_in = x_in
            else:
                own_act = jax.nn.leaky_relu(saved_out[-1], 0.2).astype(jnp.bfloat16)
                layer_in = lax.all_gather(own_act, "model", axis=1, tiled=True)
            y_val = jnp.einsum("bi,oi->bo", layer_in, weight, preferred_element_type=jnp.float32) / sigma_val
            saved_in.append(layer_in)
            saved_out.append(y_val)
            layer_stats.append((s_vec / sigma_val, v_vec, sigma_val))
        residual = saved_out[2] - target.astype(jnp.float32)
        loss_val = 0.5 / batch_total * lax.psum(jnp.sum(residual * residual), ("data", "model"))
        grad_y = residual / batch_total
        grads_w = [None, None, None]
        for layer_idx in (2, 1, 0):
            weight = weights[layer_idx]
            u_next, v_vec, sigma_val = layer_stats[layer_idx]
            grad_b = grad_y.astype(jnp.bfloat16)
            corr_sum = lax.psum(jnp.sum(grad_y * saved_out[layer_idx]), ("data", "model"))
            g_part = jnp.einsum("bo,bi->oi", grad_b, saved_in[layer_idx], preferred_element_type=jnp.float32)
            g_mat = lax.psum(g_part, "data")
            grads_w[layer_idx] = g_mat / sigma_val - (corr_sum / sigma_val) * (u_next[:, None] * v_vec[None, :])
            x_part = (jnp.dot(grad_b, weight, preferred_element_type=jnp.float32) / sigma_val).astype(jnp.bfloat16)
            if layer_idx > 0:
                own_grad = lax.psum_scatter(x_part, "model", scatter_dimension=1, tiled=True)
                grad_y = own_grad.astype(jnp.float32) * jnp.where(saved_out[layer_idx - 1] > 0, 1.0, 0.2)
            else:
                grad_x = lax.psum(x_part, "model")
        return (loss_val.reshape(1), grad_x, grads_w[0], grads_w[1], grads_w[2],
                layer_stats[0][0], layer_stats[1][0], layer_stats[2][0],
                layer_stats[0][1], layer_stats[1][1], layer_stats[2][1],
                jnp.stack([layer_stats[0][2], layer_stats[1][2], layer_stats[2][2]]))

    in_specs = (batch_spec, row_spec, row_spec, row_spec, vec_spec, vec_spec, vec_spec, target_spec)
    out_specs = (part_spec, batch_spec, row_spec, row_spec, row_spec, vec_spec, vec_spec, vec_spec, part_spec, part_spec, part_spec, part_spec)
    return jax.shard_map(local_step, mesh=mesh, in_specs=in_specs, out_specs=out_specs, check_vma=False)
```

profile of v0, /device:TPU:97, one launch (start us, length us, event | category | flops | bytes accessed | tf_op | source)
XLA Modules:
  0.0 781.1 jit_solution(3507898960754282807)
XLA Ops:
  7.2 0.1 all-gather.3.cloned.1.call-start
  7.3 1.2 fusion.8
  8.5 0.9 fusion.6
  9.4 1.2 fusion.4
  10.5 24.0 %all-reduce.2 = (f32[1024]{0:T(1024)S(1)}, f32[1024]{0:T(1024)S(1)}, f32[1024]{0:T(1024)S(1)}) all-reduce(f32[1024]{0:T(1024)S(1)} %bitcast.57, f32[1024]{0:T(1024)S(1)} %bitcast.58, f32[1024]{0:T(1024)S(1)} %bitcast.59), channel_id=1, replica_groups=mesh['replica'=1,'data'=4,'model'=8] {'model'}, use_global_device_ids=true, to_apply=%region_0.0 | all-reduce | flops 3072 | bytes 24576 | tf_op jit(solution)/shard_map/psum | solution.py:27
  34.5 0.6 multiply_reduce_fusion.6
  35.9 0.6 copy-done.9
  36.4 2.4 multiply_reduce_fusion.9
  38.8 0.6 multiply_reduce_fusion.4
  40.9 0.6 copy-done.11
  41.4 2.4 multiply_reduce_fusion.7
  43.9 1.4 multiply_reduce_fusion.8
  45.3 16.0 %all-reduce.1 = (f32[]{:T(128)}, f32[]{:T(128)}, f32[]{:T(128)}) all-reduce(f32[]{:T(128)} %get-tuple-element.27, f32[]{:T(128)} %get-tuple-element.29, f32[]{:T(128)} %get-tuple-element.31), channel_id=1, replica_groups=mesh['replica'=1,'data'=4,'model'=8] {'model'}, use_global_device_ids=true, to_apply=%region_3.0 | all-reduce | flops 3 | bytes 24 | tf_op jit(solution)/shard_map/psum | solution.py:30
  61.9 13.0 %fusion = (bf16[8192,128]{1,0:T(8,128)(2,1)}, f32[8192,128]{1,0:T(8,128)}) fusion(f32[]{:T(128)} %sqrt.19, bf16[8192,1024]{1,0:T(8,128)(2,1)} %param.8, bf16[128,1024]{1,0:T(8,128)(2,1)} %param.9), kind=kOutput, calls=%fused_computation.8 | convolution fusion | flops 2152726528 | bytes 23330820 | tf_op jit(solution)/shard_map/bi,oi->bo/dot_general | solution.py:36
  75.0 0.1 all-gather.3.cloned.1.call-update
  75.0 0.1 all-gather.5.cloned.1.call-start
  75.8 87.3 %all-gather.3.cloned.1.call-done = bf16[8192,1024]{1,0:T(8,128)(2,1)} async-done(((bf16[8192,128]{1,0:T(8,128)(2,1)}), bf16[8192,1024]{1,0:T(8,128)(2,1)}) %all-gather.3.cloned.1.call-update) | async-done | bytes 16777232 | tf_op jit(solution)/shard_map/all_gather | solution.py:35
  163.1 13.0 %fusion.1 = (bf16[8192,128]{1,0:T(8,128)(2,1)}, f32[8192,128]{1,0:T(8,128)}) fusion(f32[]{:T(128)} %sqrt.21, bf16[8192,1024]{1,0:T(8,128)(2,1)} %all-gather.3.cloned.1.call-done, bf16[128,1024]{1,0:T(8,128)(2,1)S(1)} %copy-done), kind=kOutput, calls=%fused_computation.9 | convolution fusion | flops 2152726528 | bytes 23330820 | tf_op jit(solution)/shard_map/bi,oi->bo/dot_general | solution.py:36
  176.1 0.1 all-gather.5.cloned.1.call-update
  176.2 0.2 reduce-scatter.7.cloned.1.call-start
  177.1 87.2 %all-gather.5.cloned.1.call-done = bf16[8192,1024]{1,0:T(8,128)(2,1)} async-done(((bf16[8192,128]{1,0:T(8,128)(2,1)}), bf16[8192,1024]{1,0:T(8,128)(2,1)}) %all-gather.5.cloned.1.call-update) | async-done | bytes 16777232 | tf_op jit(solution)/shard_map/all_gather | solution.py:35
  264.3 8.9 %multiply_reduce_fusion = (f32[]{:T(128)}, f32[]{:T(128)}, f32[8192,128]{1,0:T(8,128)S(1)}) fusion(bf16[8192,128]{1,0:T(8,128)(2,1)S(1)} %copy-done.6, f32[]{:T(128)} %sqrt.23, bf16[8192,1024]{1,0:T(8,128)(2,1)} %all-gather.5.cloned.1.call-done, bf16[128,1024]{1,0:T(8,128)(2,1)S(1)} %copy-done.7), kind=kOutput, calls=%fused_computation.10 | convolution fusion | flops 2155872256 | bytes 23330828 | tf_op jit(solution)/shard_map/bi,oi->bo/dot_general | solution.py:36
  273.3 1.9 copy-done.5
  275.2 8.5 %divide_convert_fusion.2 = bf16[8192,1024]{1,0:T(8,128)(2,1)} fusion(f32[]{:T(128)} %sqrt.23, bf16[128,1024]{1,0:T(8,128)(2,1)S(1)} %copy-done.7, f32[8192,128]{1,0:T(8,128)S(1)} %get-tuple-element.37, bf16[8192,128]{1,0:T(8,128)(2,1)S(1)} %copy-done.6), kind=kOutput, calls=%fused_computation.2 | convolution fusion | flops 2168455168 | bytes 23330820 | tf_op jit(solution)/shard_map/dot_general | solution.py:52
  283.7 20.7 %copy.20 = bf16[8192,1024]{0,1:T(8,128)(2,1)} copy(bf16[8192,1024]{1,0:T(8,128)(2,1)} %divide_convert_fusion.2) | data formatting | bytes 33554432
  304.4 0.1 reduce-scatter.7.cloned.1.call-update
  304.5 0.1 reduce-scatter.9.cloned.1.call-start
  304.6 89.4 %reduce-scatter.7.cloned.1.call-done = bf16[128,8192]{1,0:T(8,128)(2,1)} async-done(((bf16[1024,8192]{1,0:T(8,128)(2,1)}), bf16[128,8192]{1,0:T(8,128)(2,1)}) %reduce-scatter.7.cloned.1.call-update) | async-done | bytes 2097168
  394.0 3.2 copy.21
  397.2 10.7 %divide_convert_fusion.1 = bf16[8192,1024]{1,0:T(8,128)(2,1)} fusion(f32[]{:T(128)} %sqrt.21, bf16[128,1024]{1,0:T(8,128)(2,1)S(1)} %copy-done, bf16[8192,128]{1,0:T(8,128)(2,1)S(1)} %copy.21, f32[8192,128]{1,0:T(8,128)} %get-tuple-element.36), kind=kOutput, calls=%fused_computation.1 | convolution fusion | flops 2169503744 | bytes 23330820 | tf_op jit(solution)/shard_map/dot_general | solution.py:52
  407.9 20.7 %copy.22 = bf16[8192,1024]{0,1:T(8,128)(2,1)} copy(bf16[8192,1024]{1,0:T(8,128)(2,1)} %divide_convert_fusion.1) | data formatting | bytes 33554432
  428.7 0.3 all-reduce.9.cloned.1.call-start
  429.0 10.9 %fusion.10 = f32[128,1024]{1,0:T(8,128)} fusion(bf16[8192,1024]{1,0:T(8,128)(2,1)} %all-gather.5.cloned.1.call-done, f32[8192,128]{1,0:T(8,128)} %copy-done.5, bf16[8192,128]{1,0:T(8,128)(2,1)} %param.15), kind=kOutput, calls=%fused_computation.45 | convolution fusion | flops 2151677952 | bytes 23592960 | tf_op jit(solution)/shard_map/bo,bi->oi/dot_general | solution.py:49
  439.9 8.9 %fusion.11 = f32[128,1024]{1,0:T(8,128)} fusion(bf16[8192,1024]{1,0:T(8,128)(2,1)} %all-gather.3.cloned.1.call-done, bf16[8192,128]{1,0:T(8,128)(2,1)S(1)} %copy.21, f32[8192,128]{1,0:T(8,128)S(1)} %copy-done.3), kind=kOutput, calls=%fused_computation.46 | convolution fusion | flops 2152726528 | bytes 23592960 | tf_op jit(solution)/shard_map/bo,bi->oi/dot_general | solution.py:49
  448.8 69.0 %reduce-scatter.9.cloned.1.call-done = bf16[128,8192]{1,0:T(8,128)(2,1)} async-done(((bf16[1024,8192]{1,0:T(8,128)(2,1)}), bf16[128,8192]{1,0:T(8,128)(2,1)}) %reduce-scatter.9.cloned.1.call-update) | async-done | bytes 2097168
  517.8 4.1 copy.23
  521.9 10.8 %fusion.14 = f32[128,1024]{1,0:T(8,128)} fusion(bf16[8192,1024]{1,0:T(8,128)(2,1)} %param.8, bf16[8192,128]{1,0:T(8,128)(2,1)} %copy.23, f32[8192,128]{1,0:T(8,128)} %get-tuple-element.34), kind=kOutput, calls=%fused_computation.47 | convolution fusion | flops 2152726528 | bytes 23592960 | tf_op jit(solution)/shard_map/bo,bi->oi/dot_general | solution.py:49
  532.8 0.3 all-reduce.7.cloned.1.call-start
  533.1 11.3 %divide_convert_fusion = bf16[8192,1024]{1,0:T(8,128)(2,1)} fusion(f32[]{:T(128)} %sqrt.19, bf16[128,1024]{1,0:T(8,128)(2,1)S(1)} %copy-done.8, bf16[8192,128]{1,0:T(8,128)(2,1)} %copy.23, f32[8192,128]{1,0:T(8,128)} %get-tuple-element.34), kind=kOutput, calls=%fused_computation | convolution fusion | flops 2169503744 | bytes 23330820 | tf_op jit(solution)/shard_map/dot_general | solution.py:52
  544.6 0.6 pad_maximum_fusion
  545.3 4.2 multiply_reduce_fusion.1
  549.5 1.7 multiply_reduce_fusion.2
  551.2 46.9 %all-reduce = (f32[]{:T(128)}, f32[]{:T(128)}, f32[]{:T(128)}, f32[]{:T(128)}) all-reduce(f32[]{:T(128)} %get-tuple-element.13, f32[]{:T(128)} %multiply_reduce_fusion.2, f32[]{:T(128)} %multiply_reduce_fusion.1, f32[]{:T(128)} %get-tuple-element.12), channel_id=1, replica_groups=mesh['replica'=1,'data'=4,'model'=8] {'data','model'}, use_global_device_ids=true, to_apply=%region_13.14 | all-reduce | flops 4 | bytes 32 | tf_op jit(solution)/shard_map/psum | solution.py:41
  600.7 2.0 multiply_subtract_fusion.2
  602.6 2.0 multiply_subtract_fusion.1
  604.6 2.0 multiply_subtract_fusion
  606.6 152.6 %all-reduce.7.cloned.1.call-done = bf16[8192,1024]{1,0:T(8,128)(2,1)} async-done(((bf16[8192,1024]{1,0:T(8,128)(2,1)}), bf16[8192,1024]{1,0:T(8,128)(2,1)}) %all-reduce.7.cloned.1.call-update) | async-done | bytes 16777232 | tf_op jit(solution)/shard_map/psum | solution.py:57
  759.2 14.0 %copy.28 = bf16[8192,1024]{1,0:T(8,128)(2,1)} copy(bf16[8192,1024]{1,0:T(8,128)(2,1)} %all-reduce.7.cloned.1.call-done) | data formatting | bytes 33554432
  (49 shorter events, 0.3 us)
Async XLA Ops:
  7.2 1.3 copy-start
  7.2 155.9 %all-gather.3.cloned.1.call-start = ((), (), s32[]{:S(2)}) async-start(), calls=%async_computation.2 | async-start | bytes 18874368 | tf_op jit(solution)/shard_map/all_gather | solution.py:35
  35.8 0.6 copy-start.9
  40.8 0.6 copy-start.11
  40.8 3.0 copy-start.13
  75.0 189.3 %all-gather.5.cloned.1.call-start = ((), (), s32[]{:S(2)}) async-start(), calls=%async_computation.3 | async-start | bytes 18874368 | tf_op jit(solution)/shard_map/all_gather | solution.py:35
  75.8 188.6 %copy-start.6 = (bf16[8192,128]{1,0:T(8,128)(2,1)S(1)}, bf16[8192,128]{1,0:T(8,128)(2,1)}, u32[]{:S(2)}) copy-start(bf16[8192,128]{1,0:T(8,128)(2,1)} %param.15) | copy-start | bytes 6291460
  75.8 188.5 %copy-start.7 = (bf16[128,1024]{1,0:T(8,128)(2,1)S(1)}, bf16[128,1024]{1,0:T(8,128)(2,1)}, u32[]{:S(2)}) copy-start(bf16[128,1024]{1,0:T(8,128)(2,1)} %param.11) | copy-start | bytes 786436
  176.2 217.8 %reduce-scatter.7.cloned.1.call-start = ((), (), s32[]{:S(2)}) async-start(), calls=%async_computation.5 | async-start | bytes 18874368
  273.3 1.9 copy-start.5
  304.5 213.3 %reduce-scatter.9.cloned.1.call-start = ((), (), s32[]{:S(2)}) async-start(), calls=%async_computation.6 | async-start | bytes 18874368
  428.7 171.9 %all-reduce.9.cloned.1.call-start = ((), (), s32[]{:S(2)}) async-start(), calls=%async_computation.7 | async-start | bytes 3145728 | tf_op jit(solution)/shard_map/psum | solution.py:50
  429.0 10.9 %copy-start.3 = (f32[8192,128]{1,0:T(8,128)S(1)}, f32[8192,128]{1,0:T(8,128)}, u32[]{:S(2)}) copy-start(f32[8192,128]{1,0:T(8,128)} %get-tuple-element.36) | copy-start | bytes 12582916
  521.9 11.2 %copy-start.8 = (bf16[128,1024]{1,0:T(8,128)(2,1)S(1)}, bf16[128,1024]{1,0:T(8,128)(2,1)}, u32[]{:S(2)}) copy-start(bf16[128,1024]{1,0:T(8,128)(2,1)} %param.9) | copy-start | bytes 786436
  532.8 226.4 %all-reduce.7.cloned.1.call-start = ((), (), s32[]{:S(2)}) async-start(), calls=%async_computation.4 | async-start | bytes 33554432 | tf_op jit(solution)/shard_map/psum | solution.py:57
  544.5 0.7 copy-start.15
  544.5 0.7 copy-start.17
  544.5 0.7 copy-start.16
  544.6 4.9 copy-start.2
  544.6 4.9 copy-start.4
  545.2 55.5 %copy-start.18 = (f32[128]{0:T(128)}, f32[128]{0:T(128)S(1)}, u32[]{:S(2)}) copy-start(f32[128]{0:T(128)S(1)} %broadcast_divide_fusion.5) | copy-start | bytes 1540
  545.2 57.4 %copy-start.19 = (f32[128]{0:T(128)}, f32[128]{0:T(128)S(1)}, u32[]{:S(2)}) copy-start(f32[128]{0:T(128)S(1)} %broadcast_divide_fusion.4) | copy-start | bytes 1540
  545.2 59.3 %copy-start.20 = (f32[128]{0:T(128)}, f32[128]{0:T(128)S(1)}, u32[]{:S(2)}) copy-start(f32[128]{0:T(128)S(1)} %broadcast_divide_fusion.3) | copy-start | bytes 1540
  549.4 51.2 %copy-start.10 = (f32[1024]{0:T(1024)S(1)}, f32[1024]{0:T(1024)}, u32[]{:S(2)}) copy-start(f32[1024]{0:T(1024)} %copy-done.9) | copy-start | bytes 12292
  549.4 53.2 %copy-start.14 = (f32[1024]{0:T(1024)S(1)}, f32[1024]{0:T(1024)}, u32[]{:S(2)}) copy-start(f32[1024]{0:T(1024)} %copy-done.13) | copy-start | bytes 12292
  549.5 55.1 %copy-start.12 = (f32[1024]{0:T(1024)S(1)}, f32[1024]{0:T(1024)}, u32[]{:S(2)}) copy-start(f32[1024]{0:T(1024)} %copy-done.11) | copy-start | bytes 12292
  759.2 14.0 %copy-start.1 = (bf16[128,1024]{1,0:T(8,128)(2,1)S(1)}, bf16[128,1024]{1,0:T(8,128)(2,1)}, u32[]{:S(2)}) copy-start(bf16[128,1024]{1,0:T(8,128)(2,1)} %param.10) | copy-start | bytes 786436
Sparse Core Ops, SparseCore 0:
  75.1 87.9 all-gather.2
  176.3 88.0 all-gather.4
  304.6 89.3 reduce-scatter.6
  428.8 88.9 reduce-scatter.8
  532.9 45.8 all-reduce.8
  581.8 177.3 all-reduce.6
where the time goes:
time: 783 us; the launch traced here: 781 us
  waiting for transfers between devices  486 us (62%)
  matrix products  106 us (14%)
  blocking collectives  86.8 us (11%)
  local copies, waits for them, and re-layouts  65.9 us (8%)
  between operations  22.2 us (3%)
  other arithmetic  13.6 us (2%)
    all_gather x2, waiting for transfers between devices, local_step(): layer_in = lax.all_gather(own_act, 'model', axis=1, tiled=True)  175 us
    unnamed x8, waiting for transfers between devices  159 us
    psum x1, waiting for transfers between devices, local_step(): grad_x = lax.psum(x_part, 'model')  153 us
    unnamed x47, local copies, waits for them, and re-layouts  65.9 us
    psum x1, blocking collectives, local_step(): lax.psum(jnp.sum(residual * residual), ('data', 'model'))  46.9 us
    dot_general x3, matrix products, local_step(): jnp.einsum('bi,oi->bo', layer_in, weight, preferred_element_type=jnp.floa...  35 us
    dot_general x3, matrix products, local_step(): jnp.einsum('bo,bi->oi', grad_b, saved_in[layer_idx], preferred_element_ty...  30.7 us
    dot_general x3, matrix products, local_step(): jnp.dot(grad_b, weight, preferred_element_type=jnp.float32) / sigma_val  30.6 us
  transfers between devices with their start and end apart: 6, of which 5 were waited for; matrix products, arithmetic and copies ran while one was open for 6% of the time, Pallas kernels for 0%

commit v1 on v0

v1 whole, which is shorter than its diff:
```python
import functools

import jax
import jax.numpy as jnp
from jax import lax
from jax.experimental import pallas as pl
from jax.experimental.pallas import tpu as pltpu
from jax.sharding import PartitionSpec as P

F32 = jnp.float32
BF16 = jnp.bfloat16
CORES = 2
LANES = 128
NBLK = 256
MESH_ID = pl.DeviceIdType.MESH


def wait_bytes(ref, sem):
    pltpu.make_async_copy(ref, ref, sem).wait()


def dot(a, b):
    return jnp.dot(a, b, preferred_element_type=F32)


def split3(a):
    hi = a.astype(BF16)
    rest = a - hi.astype(F32)
    mid = rest.astype(BF16)
    low = (rest - mid.astype(F32)).astype(BF16)
    return jnp.concatenate([hi, mid, low], axis=0)


def stack_kernel(n_model, chunk, batch_total,
                 w_ref, u_ref, x_hbm, t_hbm,
                 dx_hbm, dw_ref, small_ref,
                 W, WT, U, T, xb, x1, x2, y0, y1, e2, e1, e0, dxb, sums,
                 u_send, u_recv, w_send, w_fwd, w_d2d, wl, wr, wf, wp,
                 t_own, t_send, t_fwd, tl, tr, tf, tp,
                 x_sem, dx_loc, dx_send, dx_recv):
    n_chips = n_model // CORES
    n_layers, shard, width = w_ref.shape
    rows = x_hbm.shape[0] // CORES
    n_chunk = rows // chunk
    half = chunk // 2
    me = lax.axis_index("model")
    chip = me // CORES
    core = me % CORES
    right = (chip + 1) % n_chips
    left = (chip + n_chips - 1) % n_chips
    far = (chip + 2) % n_chips
    partner = chip * CORES + (1 - core)
    row0 = core * rows

    def dev(m):
        return {"model": m}

    def remote(src, dst, ssem, rsem, m):
        cp = pltpu.make_async_remote_copy(src_ref=src, dst_ref=dst, send_sem=ssem, recv_sem=rsem,
                                          device_id=dev(m), device_id_type=MESH_ID)
        cp.start()

    barrier = pltpu.get_barrier_semaphore()
    for step in range(1, n_model):
        pl.semaphore_signal(barrier, inc=1, device_id=dev((me + step) % n_model), device_id_type=MESH_ID)
    pl.semaphore_wait(barrier, n_model - 1)

    mrow = pl.multiple_of(me * shard, shard)
    hs = shard // 2

    def send_w(k):
        for nb, rsem in ((right, wl), (left, wr)):
            remote(w_ref.at[k], W.at[k, pl.ds(mrow, shard)], w_send.at[k], rsem.at[k], nb * CORES + core)
        remote(w_ref.at[k], W.at[k, pl.ds(mrow, shard)], w_d2d.at[k], wp.at[k], partner)

    def rows_of(c):
        return pl.multiple_of((c * CORES + core) * shard, shard)

    def forward_w(k):
        src_l = W.at[k, pl.ds(rows_of(left), shard)]
        src_r = W.at[k, pl.ds(rows_of(right), shard)]
        wait_bytes(src_l, wl.at[k])
        half_l = W.at[k, pl.ds(rows_of(left), hs)]
        remote(half_l, half_l, w_fwd.at[k], wf.at[k], right * CORES + core)
        remote(src_l, src_l, w_d2d.at[k], wp.at[k], partner)
        wait_bytes(src_r, wr.at[k])
        half_r = W.at[k, pl.ds(rows_of(right) + hs, hs)]
        remote(half_r, half_r, w_fwd.at[k], wf.at[k], left * CORES + core)
        remote(src_r, src_r, w_d2d.at[k], wp.at[k], partner)

    def finish_w(k):
        src_f = W.at[k, pl.ds(rows_of(far), shard)]
        wait_bytes(src_f, wf.at[k])
        remote(src_f, src_f, w_d2d.at[k], wp.at[k], partner)
        wait_bytes(W.at[k, pl.ds(0, n_chips * shard)], wp.at[k])

    def send_t(r):
        for c in range(CORES):
            src = t_hbm.at[pl.ds(c * rows + r * chunk, chunk)]
            dst = T.at[me, pl.ds(r * chunk, chunk)]
            for nb, rsem in ((right, tl), (left, tr)):
                remote(src, dst, t_send.at[r], rsem.at[r], nb * CORES + c)
        src = t_hbm.at[pl.ds(pl.multiple_of((1 - core) * rows + r * chunk, chunk), chunk)]
        remote(src, T.at[me, pl.ds(r * chunk, chunk)], t_send.at[r], tp.at[r], partner)

    def forward_t(r):
        wait_bytes(T.at[pl.ds(left * CORES, CORES), pl.ds(r * chunk, chunk)], tl.at[r])
        for c in range(CORES):
            ref = T.at[left * CORES + c, pl.ds(r * chunk, half)]
            remote(ref, ref, t_fwd.at[r], tf.at[r], right * CORES + core)
        wait_bytes(T.at[pl.ds(right * CORES, CORES), pl.ds(r * chunk, chunk)], tr.at[r])
        for c in range(CORES):
            ref = T.at[right * CORES + c, pl.ds(r * chunk + half, half)]
            remote(ref, ref, t_fwd.at[r], tf.at[r], left * CORES + core)

    def load_x(r, slot):
        return pltpu.make_async_copy(x_hbm.at[pl.ds(pl.multiple_of(row0 + r * chunk, chunk), chunk)],
                                     xb.at[slot], x_sem.at[slot])

    send_w(0)
    for step in range(1, n_model):
        remote(u_ref, U.at[me], u_send, u_recv, (me + step) % n_model)
    send_w(1)
    send_w(2)
    own_t = pltpu.make_async_copy(t_hbm.at[pl.ds(pl.multiple_of(row0, rows), rows)], T.at[me], t_own)
    own_t.start()
    load_x(0, 0).start()
    U[me] = u_ref[...]
    for k in range(n_layers):
        W[k, pl.ds(mrow, shard)] = w_ref[k]
    sums[...] = jnp.zeros_like(sums)
    dw_ref[...] = jnp.zeros_like(dw_ref)
    small_ref[...] = jnp.zeros_like(small_ref)
    wait_bytes(U.at[pl.ds(0, n_model - 1)], u_recv)
    wait_bytes(U.at[pl.ds(0, n_model - 1)], u_send)

    forward_w(0)
    for k in range(n_layers):
        if k + 1 < n_layers:
            forward_w(k + 1)
        else:
            send_t(0)
            send_t(1)
        finish_w(k)
        for i in range(width // NBLK):
            for j in range(width // NBLK):
                blk = W[k, i * NBLK:(i + 1) * NBLK, j * NBLK:(j + 1) * NBLK]
                WT[k, j * NBLK:(j + 1) * NBLK, i * NBLK:(i + 1) * NBLK] = blk.T
        u_all = jnp.concatenate([U[m] for m in range(n_model)], axis=1)
        p_all = dot(split3(u_all), W[k])
        p_row = p_all[k:k + 1] + p_all[8 + k:9 + k] + p_all[16 + k:17 + k]
        p_norm = jnp.sqrt(jnp.sum(p_row * p_row, axis=1, keepdims=True))
        v_row = p_row / jnp.maximum(p_norm, 1e-12)
        s_all = dot(split3(jnp.broadcast_to(v_row, (8, width))), WT[k])
        s_row = s_all[0:1] + s_all[8:9] + s_all[16:17]
        sigma = jnp.sqrt(jnp.sum(s_row * s_row, axis=1, keepdims=True))
        small_ref[k:k + 1] = v_row
        small_ref[n_layers + k:n_layers + k + 1] = s_row / sigma
        small_ref[2 * n_layers + k:2 * n_layers + k + 1] = jnp.broadcast_to(sigma, (1, width))
    for k in range(n_layers):
        wait_bytes(W.at[k, pl.ds(0, CORES * shard)], w_send.at[k])
        wait_bytes(W.at[k, pl.ds(0, shard)], w_fwd.at[k])
        wait_bytes(W.at[k, pl.ds(0, n_chips * shard)], w_d2d.at[k])
    own_t.wait()
    forward_t(0)
    inv = [1.0 / small_ref[2 * n_layers + k:2 * n_layers + k + 1, 0:1] for k in range(n_layers)]
    blocks = [slice(n * NBLK, (n + 1) * NBLK) for n in range(width // NBLK)]
    own_cols = pl.multiple_of(chip * CORES * shard, CORES * shard)

    def add_sum(i, val):
        sums[i] += jnp.sum(val.reshape(chunk // 8, 8, NBLK), axis=0)

    def body(r, carry):
        slot = r % 2
        load_x(r, slot).wait()

        @pl.when(r + 1 < n_chunk)
        def _():
            load_x(r + 1, 1 - slot).start()

        @pl.when(r + 2 < n_chunk)
        def _():
            send_t(r + 2)

        xin = xb.at[slot]
        for src, k, yk, xk in ((xin, 0, y0, x1), (x1, 1, y1, x2)):
            for blk in blocks:
                y_val = dot(src[...], WT[k, :, blk]) * inv[k]
                yk[:, blk] = y_val
                xk[:, blk] = jnp.maximum(y_val, 0.2 * y_val).astype(BF16)

        @pl.when(r + 1 < n_chunk)
        def _():
            forward_t(r + 1)

        wait_bytes(T.at[pl.ds(far * CORES, CORES), pl.ds(r * chunk, chunk)], tf.at[r])
        wait_bytes(T.at[partner, pl.ds(r * chunk, chunk)], tp.at[r])

        @pl.when(r >= 2)
        def _():
            out_wait(r - 2, slot)

        trow = pl.ds(pl.multiple_of(r * chunk, chunk), chunk)
        for n, blk in enumerate(blocks):
            y_val = dot(x2[...], WT[2, :, blk]) * inv[2]
            t_val = jnp.concatenate([T[2 * n, trow], T[2 * n + 1, trow]], axis=1).astype(F32)
            res = y_val - t_val
            add_sum(3, res * res)
            g_val = res / batch_total
            add_sum(2, g_val * y_val)
            e2[:, blk] = g_val.astype(BF16)
        for k, ek, yk, en in ((2, e2, y1, e1), (1, e1, y0, e0)):
            for blk in blocks:
                r_val = (dot(ek[...], W[k, :, blk]) * inv[k]).astype(BF16).astype(F32)
                y_val = yk[:, blk]
                g_val = jnp.where(y_val > 0, r_val, 0.2 * r_val)
                add_sum(k - 1, g_val * y_val)
                en[:, blk] = g_val.astype(BF16)
        for blk in blocks:
            dxb[slot, :, blk] = (dot(e0[...], W[0, :, blk]) * inv[0]).astype(BF16)
        out_copy(r, slot).start()
        out_remote(r, slot).start()
        for k, ek, xk in ((2, e2, x2), (1, e1, x1), (0, e0, xin)):
            e_own = ek[:, pl.ds(own_cols, CORES * shard)].T
            dw_ref[k] += dot(e_own, xk[...])
        return carry

    def out_rows(r):
        return pl.ds(pl.multiple_of(row0 + r * chunk, chunk), chunk)

    def out_copy(r, slot):
        return pltpu.make_async_copy(dxb.at[slot], dx_hbm.at[out_rows(r)], dx_loc.at[slot])

    def out_remote(r, slot):
        return pltpu.make_async_remote_copy(src_ref=dxb.at[slot], dst_ref=dx_hbm.at[out_rows(r)],
                                            send_sem=dx_send.at[slot], recv_sem=dx_recv.at[r],
                                            device_id=dev(partner), device_id_type=MESH_ID)

    def out_wait(r, slot):
        out_copy(r, slot).wait()
        out_remote(r, slot).wait_send()

    lax.fori_loop(0, n_chunk, body, 0)
    out_wait(n_chunk - 2, 0)
    out_wait(n_chunk - 1, 1)

    def drain(r, carry):
        wait_bytes(T.at[pl.ds(0, 2 * CORES + 1), pl.ds(0, chunk)], t_send.at[r])
        wait_bytes(T.at[pl.ds(0, CORES), pl.ds(0, chunk)], t_fwd.at[r])
        pltpu.make_async_copy(dxb.at[0], dxb.at[0], dx_recv.at[r]).wait()
        return carry

    lax.fori_loop(0, n_chunk, drain, 0)
    for i in range(4):
        tot = jnp.sum(jnp.sum(sums[i], axis=0, keepdims=True), axis=1, keepdims=True)
        small_ref[9 + i:10 + i] = jnp.broadcast_to(tot, (1, width))


def solution(mesh):
    data_size = mesh.shape["data"]
    n_model = mesh.shape["model"]
    row_spec = P(("replica", "model"), None)
    vec_spec = P(("replica", "model"))
    batch_spec = P(("replica", "data"), None)
    target_spec = P(("replica", "data"), "model")
    part_spec = P("replica")

    def local_step(x_in, w_in, w_mid, w_out, u_in, u_mid, u_out, target):
        rows_all, width = x_in.shape
        shard = w_in.shape[0]
        batch_total = rows_all * data_size
        rows = rows_all // CORES
        chunk = rows // 8
        n_chunk = rows // chunk
        w_all = jnp.stack([w_in, w_mid, w_out])
        u_all = jnp.concatenate([jnp.stack([u_in, u_mid, u_out]), jnp.zeros((5, shard), F32)], axis=0)
        vm = pltpu.VMEM
        dma = pltpu.SemaphoreType.DMA
        any_spec = pl.BlockSpec(memory_space=pl.ANY)
        vmem_spec = pl.BlockSpec(memory_space=pltpu.VMEM)
        dx, dw, small = pl.pallas_call(
            functools.partial(stack_kernel, n_model, chunk, batch_total),
            out_shape=(jax.ShapeDtypeStruct((rows_all, width), BF16),
                       jax.ShapeDtypeStruct((3, CORES * shard, width), F32),
                       jax.ShapeDtypeStruct((16, width), F32)),
            in_specs=[vmem_spec, vmem_spec, any_spec, any_spec],
            out_specs=(any_spec, vmem_spec, vmem_spec),
            scratch_shapes=[
                vm((3, width, width), BF16), vm((3, width, width), BF16),
                vm((n_model, 8, shard), F32), vm((n_model, rows, shard), BF16),
                vm((2, chunk, width), BF16), vm((chunk, width), BF16), vm((chunk, width), BF16),
                vm((chunk, width), F32), vm((chunk, width), F32),
                vm((chunk, width), BF16), vm((chunk, width), BF16), vm((chunk, width), BF16),
                vm((2, chunk, width), BF16), vm((4, 8, NBLK), F32),
                dma, dma, dma((3,)), dma((3,)), dma((3,)), dma((3,)), dma((3,)), dma((3,)), dma((3,)),
                dma, dma((n_chunk,)), dma((n_chunk,)), dma((n_chunk,)), dma((n_chunk,)), dma((n_chunk,)), dma((n_chunk,)),
                dma((2,)), dma((2,)), dma((2,)), dma((n_chunk,))],
            compiler_params=pltpu.CompilerParams(collective_id=0, has_side_effects=True,
                                                 vmem_limit_bytes=60 * 1024 * 1024),
        )(w_all, u_all, x_in, target)

        me = lax.axis_index("model")
        core = me % CORES
        v_rows = small[0:3]
        sigma = small[6:9, 0]
        scal = small[9:13, 0]
        swap = [(i, i ^ 1) for i in range(n_model)]
        mine = lax.dynamic_slice_in_dim(dw, core * shard, shard, axis=1)
        other = lax.dynamic_slice_in_dim(dw, (1 - core) * shard, shard, axis=1)
        mine = mine + lax.ppermute(other, "model", swap)
        g_mat = lax.psum(mine, "data")
        scal = lax.psum(scal, ("data", "model")) * (CORES / n_model)
        u_next = lax.dynamic_slice_in_dim(small[3:6], me * shard, shard, axis=1)
        dws = [g_mat[k] / sigma[k] - (scal[k] / sigma[k]) * (u_next[k][:, None] * v_rows[k][None, :]) for k in range(3)]
        loss_val = 0.5 / batch_total * scal[3]
        return (loss_val.reshape(1), dx, dws[0], dws[1], dws[2],
                u_next[0], u_next[1], u_next[2], v_rows[0], v_rows[1], v_rows[2], sigma)

    in_specs = (batch_spec, row_spec, row_spec, row_spec, vec_spec, vec_spec, vec_spec, target_spec)
    out_specs = (part_spec, batch_spec, row_spec, row_spec, row_spec, vec_spec, vec_spec, vec_spec, part_spec, part_spec, part_spec, part_spec)
    return jax.shard_map(local_step, mesh=mesh, in_specs=in_specs, out_specs=out_specs, check_vma=False)
```

time: 783 us -> 227 us (0.29)
  waiting for transfers between devices: 486 us -> 3.19 us
  Pallas kernels: 0 us -> 125 us
  matrix products: 106 us -> 0 us
  local copies, waits for them, and re-layouts: 65.9 us -> 19.7 us
  blocking collectives: 86.8 us -> 48.4 us
    all_gather x2 -> x0, waiting for transfers between devices: 175 us -> none  [local_step(): layer_in = lax.all_gather(own_act, 'model', axis=1, tiled=True)]
    unnamed x8 -> x1, waiting for transfers between devices: 159 us -> 0.05 us
    psum x2 -> x1, waiting for transfers between devices: 153 us -> 0.02 us  [local_step(): g_mat = lax.psum(mine, 'data')]
    pallas_call x0 -> x1, Pallas kernels: none -> 125 us  [local_step(): pl.pallas_call(functools.partial(stack_kernel, n_model, chunk, batch_tota...]
    dot_general x15 -> x0, matrix products: 106 us -> none  [the longest x3 35 us: local_step(): jnp.einsum('bi,oi->bo', layer_in, weight, preferred_element_type=jnp.floa...]
    unnamed x47 -> x23, local copies, waits for them, and re-layouts: 65.9 us -> 14.7 us
    psum x3 -> x1, blocking collectives: 86.8 us -> 48.4 us  [local_step(): scal = lax.psum(scal, ('data', 'model')) * (CORES / n_model)]
  transfers between devices with their start and end apart: 6 -> 2, of which waited for: 5 -> 1; matrix products, arithmetic and copies ran while one was open for 6% -> 1% of each run, Pallas kernels for 0% -> 0%
where the time goes in v1:
time: 227 us; the launch traced here: 226 us
  Pallas kernels  125 us (55%)
  blocking collectives  48.4 us (21%)
  between operations  19.9 us (9%)
  local copies, waits for them, and re-layouts  19.7 us (9%)
  other arithmetic  10 us (4%)
  waiting for transfers between devices  3.19 us (1%)
    pallas_call x1, Pallas kernels, local_step(): pl.pallas_call(functools.partial(stack_kernel, n_model, chunk, batch_tota...  125 us
    psum x1, blocking collectives, local_step(): scal = lax.psum(scal, ('data', 'model')) * (CORES / n_model)  48.4 us
    unnamed x23, local copies, waits for them, and re-layouts  14.7 us
  transfers between devices with their start and end apart: 2, of which 1 were waited for; matrix products, arithmetic and copies ran while one was open for 1% of the time, Pallas kernels for 0%

profile of v1, /device:TPU:97, one launch (start us, length us, event | category | flops | bytes accessed | tf_op | source)
XLA Modules:
  0.0 226.1 jit_solution(9633263708137286197)
XLA Ops:
  7.2 0.0 copy-start.10
  7.2 0.0 copy-start.9
  7.2 0.0 copy-start.8
  7.2 0.1 all-reduce.2.cloned.1.call-start
  7.3 0.1 pad.3.clone
  7.4 2.1 pad_maximum_fusion.w_ref
  9.5 0.0 copy-done.10
  9.5 0.0 copy-done.9
  9.5 0.0 copy-done.8
  9.5 0.7 maximum_maximum_fusion.u_ref
  10.1 124.6 %shard_map.175 = (bf16[8192,1024]{1,0:T(8,128)(2,1)}, f32[3,256,1024]{2,1,0:T(8,128)}, f32[16,1024]{1,0:T(8,128)}) custom-call(bf16[3,128,1024]{2,1,0:T(8,128)(2,1)} %pad_maximum_fusion.w_ref, f32[8,128]{1,0:T(8,128)} %maximum_maximum_fusion.u_ref, bf16[8192,1024]{1,0:T(8,128)(2,1)} %x_hbm.1, bf16[8192,128]{1,0:T(8,128)(2,1)} %t_hbm.1), custom_call_target="tpu_custom_call" | custom-call | tf_op jit(solution)/shard_map/pallas_call | solution.py:281
  134.7 0.0 copy-start
  134.7 2.9 %constant_dynamic-slice_fusion.1 = f32[3,128,1024]{2,1,0:T(8,128)} fusion(f32[3,256,1024]{2,1,0:T(8,128)} %get-tuple-element.17, s32[]{:T(128)S(6)} %select_n.18), kind=kLoop, calls=%fused_computation.15 | loop fusion | bytes 3145732 | tf_op jit(solution)/shard_map/dynamic_slice | solution.py:309
  137.6 0.2 collective-permute-start
  137.9 3.1 %collective-permute-done = f32[3,128,1024]{2,1,0:T(8,128)} collective-permute-done((f32[3,128,1024]{2,1,0:T(8,128)}, f32[3,128,1024]{2,1,0:T(8,128)}, u32[]{:S(2)}, u32[]{:S(2)}) %collective-permute-start) | collective-permute-done | bytes 1572896 | tf_op jit(solution)/shard_map/ppermute | solution.py:310
  141.0 0.0 copy-done
  141.0 2.8 %dynamic-slice_add_fusion = f32[3,128,1024]{2,1,0:T(8,128)} fusion(f32[3,128,1024]{2,1,0:T(8,128)} %collective-permute-done, f32[3,256,1024]{2,1,0:T(8,128)S(1)} %copy-done, s32[]{:T(128)S(6)} %select_n.17), kind=kLoop, calls=%fused_computation | loop fusion | flops 393216 | bytes 4718596 | tf_op jit(solution)/shard_map/add | solution.py:310
  143.8 0.0 copy-start.1
  143.8 0.1 all-reduce.2.cloned.1.call-update
  143.8 0.8 copy-done.1
  144.6 0.1 slice_reduce_fusion.1
  144.7 48.4 %psum.14 = f32[4]{0:T(128)S(1)} all-reduce(f32[4]{0:T(128)S(1)} %slice_reduce_fusion.1), channel_id=1, replica_groups=mesh['replica'=1,'data'=4,'model'=8] {'data','model'}, use_global_device_ids=true, to_apply=%region_0.1 | all-reduce | flops 4 | bytes 32 | tf_op jit(solution)/shard_map/psum | solution.py:312
  193.2 0.6 fusion.8
  193.8 0.6 fusion.6
  199.0 0.6 slice_reduce_fusion
  199.6 0.0 copy-start.5
  199.6 0.0 copy-start.6
  199.6 0.0 copy-start.7
  199.6 0.0 copy-start.2
  199.6 0.0 copy-start.3
  199.6 0.0 copy-start.4
  199.6 0.0 all-reduce.2.cloned.1.call-done
  199.7 4.5 %fusion.1 = (f32[128,1024]{1,0:T(8,128)}, f32[128,1024]{1,0:T(8,128)}, f32[128,1024]{1,0:T(8,128)}) fusion(f32[3,128,1024]{2,1,0:T(8,128)} %all-reduce.2.cloned.1.call-done, f32[1024]{0:T(1024)S(1)} %bitcast.36, f32[128]{0:T(128)S(1)} %get-tuple-element.53, f32[]{:T(128)S(6)} %div.47, f32[]{:T(128)} %bitcast.16, f32[1024]{0:T(1024)S(1)} %bitcast.38, ...), kind=kLoop, calls=%fused_computation.4 | loop fusion | flops 1572864 | bytes 3159576 | tf_op jit(solution)/shard_map/sub | solution.py:314
  204.2 0.0 copy-done.5
  204.2 0.0 copy-done.6
  204.2 0.0 copy-done.7
  204.2 0.0 copy-done.2
  204.2 0.0 copy-done.3
  204.2 0.0 copy-done.4
  204.2 13.9 %copy.22 = bf16[8192,1024]{1,0:T(8,128)(2,1)} copy(bf16[8192,1024]{1,0:T(8,128)(2,1)} %get-tuple-element.47) | data formatting | bytes 33554432
  (6 shorter events, 0.0 us)
Async XLA Ops:
  7.2 2.3 %copy-start.10 = (f32[128]{0:T(128)S(1)}, f32[128]{0:T(128)}, u32[]{:S(2)}) copy-start(f32[128]{0:T(128)} %param.12) | copy-start | bytes 1540
  7.2 2.3 %copy-start.9 = (f32[128]{0:T(128)S(1)}, f32[128]{0:T(128)}, u32[]{:S(2)}) copy-start(f32[128]{0:T(128)} %param.13) | copy-start | bytes 1540
  7.2 2.3 %copy-start.8 = (f32[128]{0:T(128)S(1)}, f32[128]{0:T(128)}, u32[]{:S(2)}) copy-start(f32[128]{0:T(128)} %param.14) | copy-start | bytes 1540
  7.2 192.4 %all-reduce.2.cloned.1.call-start = ((), (), s32[]{:S(2)}) async-start(), calls=%async_computation | async-start | bytes 3145728 | tf_op jit(solution)/shard_map/psum | solution.py:311
  134.7 6.3 %copy-start = (f32[3,256,1024]{2,1,0:T(8,128)S(1)}, f32[3,256,1024]{2,1,0:T(8,128)}, u32[]{:S(2)}) copy-start(f32[3,256,1024]{2,1,0:T(8,128)} %get-tuple-element.17) | copy-start | bytes 9437188
  137.6 3.4 %collective-permute-start = (f32[3,128,1024]{2,1,0:T(8,128)}, f32[3,128,1024]{2,1,0:T(8,128)}, u32[]{:S(2)}, u32[]{:S(2)}) collective-permute-start(f32[3,128,1024]{2,1,0:T(8,128)} %constant_dynamic-slice_fusion.1), channel_id=1, source_target_pairs={{0,1},{1,0},{2,3},{3,2},{4,5},{5,4},{6,7},{7,6},{8,9},{9,8},{10,11... | collective-permute-start | bytes 4718600 | tf_op jit(solution)/shard_map/ppermute | solution.py:310
  143.8 0.8 copy-start.1
  199.6 4.6 %copy-start.5 = (f32[128]{0:T(128)}, f32[128]{0:T(128)S(1)}, u32[]{:S(2)}) copy-start(f32[128]{0:T(128)S(1)} %get-tuple-element.53) | copy-start | bytes 1540
  199.6 4.6 %copy-start.6 = (f32[128]{0:T(128)}, f32[128]{0:T(128)S(1)}, u32[]{:S(2)}) copy-start(f32[128]{0:T(128)S(1)} %get-tuple-element.52) | copy-start | bytes 1540
  199.6 4.6 %copy-start.7 = (f32[128]{0:T(128)}, f32[128]{0:T(128)S(1)}, u32[]{:S(2)}) copy-start(f32[128]{0:T(128)S(1)} %get-tuple-element.51) | copy-start | bytes 1540
  199.6 4.6 %copy-start.2 = (f32[1,1024]{1,0:T(1,128)}, f32[1,1024]{1,0:T(1,128)S(1)}, u32[]{:S(2)}) copy-start(f32[1,1024]{1,0:T(1,128)S(1)} %get-tuple-element.24) | copy-start | bytes 12292
  199.6 4.6 %copy-start.3 = (f32[1,1024]{1,0:T(1,128)}, f32[1,1024]{1,0:T(1,128)S(1)}, u32[]{:S(2)}) copy-start(f32[1,1024]{1,0:T(1,128)S(1)} %get-tuple-element.25) | copy-start | bytes 12292
  199.6 4.6 %copy-start.4 = (f32[1,1024]{1,0:T(1,128)}, f32[1,1024]{1,0:T(1,128)S(1)}, u32[]{:S(2)}) copy-start(f32[1,1024]{1,0:T(1,128)S(1)} %get-tuple-element.26) | copy-start | bytes 12292
Sparse Core Ops, SparseCore 0:
  144.0 47.2 all-reduce.1

commit v2 on v1

--- a/solution.py
+++ b/solution.py
@@ -31,13 +31,14 @@
     return jnp.concatenate([hi, mid, low], axis=0)
 
 
-def stack_kernel(n_model, chunk, batch_total,
+def stack_kernel(n_model, n_data, chunk, batch_total,
                  w_ref, u_ref, x_hbm, t_hbm,
-                 dx_hbm, dw_ref, small_ref,
-                 W, WT, U, T, xb, x1, x2, y0, y1, e2, e1, e0, dxb, sums,
+                 dx_hbm, g_ref, small_ref,
+                 dw_ref, pair, far_l, far_r, near_l, near_r, tiles, W, WT, U, T, xb, x1, x2, y0, y1, e2, e1, e0, dxb, sums,
                  u_send, u_recv, w_send, w_fwd, w_d2d, wl, wr, wf, wp,
                  t_own, t_send, t_fwd, tl, tr, tf, tp,
-                 x_sem, dx_loc, dx_send, dx_recv):
+                 x_sem, dx_loc, dx_send, dx_recv,
+                 p_send, p_recv, fl, fr, f_send, nl, nr, n_send, gl, gr, gf, g_send, gf_send, s_send, s_recv):
     n_chips = n_model // CORES
     n_layers, shard, width = w_ref.shape
     rows = x_hbm.shape[0] // CORES
@@ -60,10 +61,19 @@
                                           device_id=dev(m), device_id_type=MESH_ID)
         cp.start()
 
+    my_data = lax.axis_index("data")
+
+    def cell(d, m):
+        return {"data": d, "model": m}
+
+    column = [(step, c) for step in range(1, n_data) for c in (core, 1 - core)]
     barrier = pltpu.get_barrier_semaphore()
     for step in range(1, n_model):
         pl.semaphore_signal(barrier, inc=1, device_id=dev((me + step) % n_model), device_id_type=MESH_ID)
-    pl.semaphore_wait(barrier, n_model - 1)
+    for step, c in column:
+        pl.semaphore_signal(barrier, inc=1, device_id=cell((my_data + step) % n_data, chip * CORES + c),
+                            device_id_type=MESH_ID)
+    pl.semaphore_wait(barrier, n_model - 1 + len(column))
 
     mrow = pl.multiple_of(me * shard, shard)
     hs = shard // 2
@@ -130,6 +140,7 @@
         W[k, pl.ds(mrow, shard)] = w_ref[k]
     sums[...] = jnp.zeros_like(sums)
     dw_ref[...] = jnp.zeros_like(dw_ref)
+    tiles[my_data * CORES + core] = jnp.zeros((8, LANES), F32)
     small_ref[...] = jnp.zeros_like(small_ref)
     wait_bytes(U.at[pl.ds(0, n_model - 1)], u_recv)
     wait_bytes(U.at[pl.ds(0, n_model - 1)], u_send)
@@ -241,6 +252,66 @@
         out_remote(r, slot).wait_send()
 
     lax.fori_loop(0, n_chunk, body, 0)
+
+    for i in range(4):
+        tot = jnp.sum(jnp.sum(sums[i], axis=0, keepdims=True), axis=1, keepdims=True)
+        tiles[my_data * CORES + core, i:i + 1] = jnp.broadcast_to(tot, (1, LANES))
+    mine = tiles.at[my_data * CORES + core]
+
+    def remote_to(src, dst, ssem, rsem, device):
+        pltpu.make_async_remote_copy(src_ref=src, dst_ref=dst, send_sem=ssem, recv_sem=rsem,
+                                     device_id=device, device_id_type=MESH_ID).start()
+
+    order = (2, 1, 0)
+    mine_rows = pl.multiple_of(core * shard, shard)
+    other_rows = pl.multiple_of((1 - core) * shard, shard)
+    qrows = shard // n_data
+    hrows = qrows // 2
+    up = (my_data + 1) % n_data
+    down = (my_data + n_data - 1) % n_data
+    opp = (my_data + 2) % n_data
+    to_up, to_down = {"data": up}, {"data": down}
+
+    def quarter(d, off, n):
+        return pl.ds(pl.multiple_of(d * qrows + off, 8), n)
+
+    def acc_quarter(d, off, n):
+        return pl.ds(pl.multiple_of(mine_rows + d * qrows + off, 8), n)
+
+    for k in order:
+        remote_to(dw_ref.at[k, pl.ds(other_rows, shard)], pair.at[k], p_send.at[k], p_recv.at[k], dev(partner))
+    remote_to(mine, mine, s_send, s_recv, dev(partner))
+    for step, c in column:
+        remote_to(mine, mine, s_send, s_recv, cell((my_data + step) % n_data, chip * CORES + c))
+    for k in order:
+        wait_bytes(pair.at[k], p_recv.at[k])
+        dw_ref[k, pl.ds(mine_rows, shard)] += pair[k]
+        remote_to(dw_ref.at[k, acc_quarter(opp, 0, hrows)], far_l.at[k], f_send.at[k], fl.at[k], to_up)
+        remote_to(dw_ref.at[k, acc_quarter(opp, hrows, hrows)], far_r.at[k], f_send.at[k], fr.at[k], to_down)
+        remote_to(dw_ref.at[k, acc_quarter(up, hrows, hrows)], near_l.at[k, pl.ds(hrows, hrows)], n_send.at[k], nl.at[k], to_up)
+        remote_to(dw_ref.at[k, acc_quarter(down, 0, hrows)], near_r.at[k, pl.ds(0, hrows)], n_send.at[k], nr.at[k], to_down)
+    for k in order:
+        wait_bytes(far_l.at[k], fl.at[k])
+        dw_ref[k, acc_quarter(up, 0, hrows)] += far_l[k]
+        remote_to(dw_ref.at[k, acc_quarter(up, 0, hrows)], near_l.at[k, pl.ds(0, hrows)], n_send.at[k], nl.at[k], to_up)
+        wait_bytes(far_r.at[k], fr.at[k])
+        dw_ref[k, acc_quarter(down, hrows, hrows)] += far_r[k]
+        remote_to(dw_ref.at[k, acc_quarter(down, hrows, hrows)], near_r.at[k, pl.ds(hrows, hrows)], n_send.at[k], nr.at[k], to_down)
+    for k in order:
+        wait_bytes(near_l.at[k], nl.at[k])
+        wait_bytes(near_r.at[k], nr.at[k])
+        g_ref[k, quarter(my_data, 0, qrows)] = dw_ref[k, acc_quarter(my_data, 0, qrows)] + near_l[k] + near_r[k]
+        ref = g_ref.at[k, quarter(my_data, 0, qrows)]
+        remote_to(ref, ref, g_send.at[k], gl.at[k], to_up)
+        remote_to(ref, ref, g_send.at[k], gr.at[k], to_down)
+    for k in order:
+        wait_bytes(g_ref.at[k, quarter(down, 0, qrows)], gl.at[k])
+        ref = g_ref.at[k, quarter(down, 0, hrows)]
+        remote_to(ref, ref, gf_send.at[k], gf.at[k], to_up)
+        wait_bytes(g_ref.at[k, quarter(up, 0, qrows)], gr.at[k])
+        ref = g_ref.at[k, quarter(up, hrows, hrows)]
+        remote_to(ref, ref, gf_send.at[k], gf.at[k], to_down)
+
     out_wait(n_chunk - 2, 0)
     out_wait(n_chunk - 1, 1)
 
@@ -251,9 +322,19 @@
         return carry
 
     lax.fori_loop(0, n_chunk, drain, 0)
-    for i in range(4):
-        tot = jnp.sum(jnp.sum(sums[i], axis=0, keepdims=True), axis=1, keepdims=True)
-        small_ref[9 + i:10 + i] = jnp.broadcast_to(tot, (1, width))
+    wait_bytes(tiles.at[pl.ds(0, len(column) + 1)], s_recv)
+    wait_bytes(tiles.at[pl.ds(0, len(column) + 1)], s_send)
+    total = tiles[0]
+    for n in range(1, n_data * CORES):
+        total = total + tiles[n]
+    small_ref[9:13] = jnp.concatenate([total[0:4]] * (width // LANES), axis=1)
+    for k in order:
+        wait_bytes(g_ref.at[k, quarter(opp, 0, qrows)], gf.at[k])
+        wait_bytes(pair.at[k], p_send.at[k])
+        wait_bytes(near_l.at[k], f_send.at[k])
+        wait_bytes(pair.at[k, pl.ds(0, 2 * qrows)], n_send.at[k])
+        wait_bytes(pair.at[k, pl.ds(0, 2 * qrows)], g_send.at[k])
+        wait_bytes(near_l.at[k], gf_send.at[k])
 
 
 def solution(mesh):
@@ -278,14 +359,18 @@
         dma = pltpu.SemaphoreType.DMA
         any_spec = pl.BlockSpec(memory_space=pl.ANY)
         vmem_spec = pl.BlockSpec(memory_space=pltpu.VMEM)
-        dx, dw, small = pl.pallas_call(
-            functools.partial(stack_kernel, n_model, chunk, batch_total),
+        dx, g_mat, small = pl.pallas_call(
+            functools.partial(stack_kernel, n_model, data_size, chunk, batch_total),
             out_shape=(jax.ShapeDtypeStruct((rows_all, width), BF16),
-                       jax.ShapeDtypeStruct((3, CORES * shard, width), F32),
+                       jax.ShapeDtypeStruct((3, shard, width), F32),
                        jax.ShapeDtypeStruct((16, width), F32)),
             in_specs=[vmem_spec, vmem_spec, any_spec, any_spec],
             out_specs=(any_spec, vmem_spec, vmem_spec),
             scratch_shapes=[
+                vm((3, CORES * shard, width), F32), vm((3, shard, width), F32),
+                vm((3, shard // data_size // 2, width), F32), vm((3, shard // data_size // 2, width), F32),
+                vm((3, shard // data_size, width), F32), vm((3, shard // data_size, width), F32),
+                vm((data_size * CORES, 8, LANES), F32),
                 vm((3, width, width), BF16), vm((3, width, width), BF16),
                 vm((n_model, 8, shard), F32), vm((n_model, rows, shard), BF16),
                 vm((2, chunk, width), BF16), vm((chunk, width), BF16), vm((chunk, width), BF16),
@@ -294,22 +379,16 @@
                 vm((2, chunk, width), BF16), vm((4, 8, NBLK), F32),
                 dma, dma, dma((3,)), dma((3,)), dma((3,)), dma((3,)), dma((3,)), dma((3,)), dma((3,)),
                 dma, dma((n_chunk,)), dma((n_chunk,)), dma((n_chunk,)), dma((n_chunk,)), dma((n_chunk,)), dma((n_chunk,)),
-                dma((2,)), dma((2,)), dma((2,)), dma((n_chunk,))],
+                dma((2,)), dma((2,)), dma((2,)), dma((n_chunk,)),
+                *[dma((3,)) for _ in range(13)], dma, dma],
             compiler_params=pltpu.CompilerParams(collective_id=0, has_side_effects=True,
                                                  vmem_limit_bytes=60 * 1024 * 1024),
         )(w_all, u_all, x_in, target)
 
         me = lax.axis_index("model")
-        core = me % CORES
         v_rows = small[0:3]
         sigma = small[6:9, 0]
         scal = small[9:13, 0]
-        swap = [(i, i ^ 1) for i in range(n_model)]
-        mine = lax.dynamic_slice_in_dim(dw, core * shard, shard, axis=1)
-        other = lax.dynamic_slice_in_dim(dw, (1 - core) * shard, shard, axis=1)
-        mine = mine + lax.ppermute(other, "model", swap)
-        g_mat = lax.psum(mine, "data")
-        scal = lax.psum(scal, ("data", "model")) * (CORES / n_model)
         u_next = lax.dynamic_slice_in_dim(small[3:6], me * shard, shard, axis=1)
         dws = [g_mat[k] / sigma[k] - (scal[k] / sigma[k]) * (u_next[k][:, None] * v_rows[k][None, :]) for k in range(3)]
         loss_val = 0.5 / batch_total * scal[3]

time: 227 us -> 188 us (0.83)
  blocking collectives: 48.4 us -> 0 us
  Pallas kernels: 125 us -> 154 us
  between operations: 19.9 us -> 6.5 us
  waiting for transfers between devices: 3.19 us -> 0 us
    psum x1 -> x0, blocking collectives: 48.4 us -> none  [local_step(): scal = lax.psum(scal, ('data', 'model')) * (CORES / n_model)]
    pallas_call x1, Pallas kernels: 125 us -> 154 us  [local_step(): pl.pallas_call(functools.partial(stack_kernel, n_model, data_size, chunk,...]
    ppermute x1 -> x0, waiting for transfers between devices: 3.12 us -> none  [local_step(): mine = mine + lax.ppermute(other, 'model', swap)]
    dynamic_slice x1 -> x0, local copies, waits for them, and re-layouts: 2.89 us -> none  [local_step(): other = lax.dynamic_slice_in_dim(dw, (1 - core) * shard, shard, axis=1)]
    add x1 -> x0, other arithmetic: 2.81 us -> none  [local_step(): mine = mine + lax.ppermute(other, 'model', swap)]
    unnamed x23 -> x13, local copies, waits for them, and re-layouts: 14.7 us -> 13.9 us
  transfers between devices with their start and end apart: 2 -> 0, of which waited for: 1 -> 0; matrix products, arithmetic and copies ran while one was open for 1% -> 0% of each run, Pallas kernels for 0% -> 0%
where the time goes in v2:
time: 188 us; the launch traced here: 187 us
  Pallas kernels  154 us (82%)
  local copies, waits for them, and re-layouts  18.4 us (10%)
  other arithmetic  8.02 us (4%)
  between operations  6.5 us (3%)
    pallas_call x1, Pallas kernels, local_step(): pl.pallas_call(functools.partial(stack_kernel, n_model, data_size, chunk,...  154 us
    unnamed x13, local copies, waits for them, and re-layouts  13.9 us
    sub x1, other arithmetic, local_step(): g_mat[k] / sigma[k]  4.6 us

profile of v2, /device:TPU:97, one launch (start us, length us, event | category | flops | bytes accessed | tf_op | source)
XLA Modules:
  0.0 187.4 jit_solution(11591474444347147623)
XLA Ops:
  0.6 2.1 %pad_maximum_fusion.w_ref = bf16[3,128,1024]{2,1,0:T(8,128)(2,1)} fusion(bf16[1,128,1024]{2,1,0:T(8,128)(2,1)} %bitcast.28, bf16[1,128,1024]{2,1,0:T(8,128)(2,1)} %bitcast.29, bf16[1,128,1024]{2,1,0:T(8,128)(2,1)} %bitcast.30), kind=kLoop, calls=%fused_computation | loop fusion | flops 786432 | bytes 1572864 | tf_op jit(solution)/shard_map/stack | solution.py:356
  2.7 0.1 pad.3.clone
  2.8 1.3 maximum_maximum_fusion.u_ref
  4.1 154.5 %shard_map.175 = (bf16[8192,1024]{1,0:T(8,128)(2,1)}, f32[3,128,1024]{2,1,0:T(8,128)}, f32[16,1024]{1,0:T(8,128)}) custom-call(bf16[3,128,1024]{2,1,0:T(8,128)(2,1)} %pad_maximum_fusion.w_ref, f32[8,128]{1,0:T(8,128)} %maximum_maximum_fusion.u_ref, bf16[8192,1024]{1,0:T(8,128)(2,1)} %x_hbm.1, bf16[8192,128]{1,0:T(8,128)(2,1)} %t_hbm.1), custom_call_target="tpu_custom_call" | custom-call | tf_op jit(solution)/shard_map/pallas_call | solution.py:362
  158.6 1.4 fusion
  164.0 0.8 slice.86
  164.8 0.0 copy-start.3
  164.8 0.0 copy-start.4
  164.8 0.0 copy-start.5
  164.9 0.9 fusion.1
  165.7 0.0 copy-start
  165.7 0.0 copy-start.1
  165.8 0.0 copy-start.2
  165.8 4.6 %bitcast_subtract_fusion = (f32[128,1024]{1,0:T(8,128)}, f32[128,1024]{1,0:T(8,128)}, f32[128,1024]{1,0:T(8,128)}) fusion(f32[3,128,1024]{2,1,0:T(8,128)} %get-tuple-element.17, f32[1024]{0:T(1024)S(1)} %bitcast.31, f32[128]{0:T(128)S(1)} %get-tuple-element.53, f32[]{:T(128)S(6)} %div.47, f32[]{:T(128)} %bitcast.17, f32[1024]{0:T(1024)S(1)} %bitcast.33, ...), kind=kLoop, calls=%fused_computation.1 | loop fusion | flops 1572864 | bytes 3159576 | tf_op jit(solution)/shard_map/sub | solution.py:393
  171.0 1.3 slice_reduce_fusion
  172.3 13.9 %copy.21 = bf16[8192,1024]{1,0:T(8,128)(2,1)} copy(bf16[8192,1024]{1,0:T(8,128)(2,1)} %get-tuple-element.47) | data formatting | bytes 33554432
  186.2 0.0 copy-done.3
  186.2 0.0 copy-done.4
  186.2 0.0 copy-done.5
  186.2 0.0 copy-done
  186.2 0.0 copy-done.1
  186.3 0.0 copy-done.2
  (3 shorter events, 0.0 us)
Async XLA Ops:
  164.8 21.4 %copy-start.3 = (f32[128]{0:T(128)}, f32[128]{0:T(128)S(1)}, u32[]{:S(2)}) copy-start(f32[128]{0:T(128)S(1)} %get-tuple-element.53) | copy-start | bytes 1540
  164.8 21.4 %copy-start.4 = (f32[128]{0:T(128)}, f32[128]{0:T(128)S(1)}, u32[]{:S(2)}) copy-start(f32[128]{0:T(128)S(1)} %get-tuple-element.52) | copy-start | bytes 1540
  164.8 21.4 %copy-start.5 = (f32[128]{0:T(128)}, f32[128]{0:T(128)S(1)}, u32[]{:S(2)}) copy-start(f32[128]{0:T(128)S(1)} %get-tuple-element.51) | copy-start | bytes 1540
  165.7 20.5 %copy-start = (f32[1,1024]{1,0:T(1,128)}, f32[1,1024]{1,0:T(1,128)S(1)}, u32[]{:S(2)}) copy-start(f32[1,1024]{1,0:T(1,128)S(1)} %get-tuple-element.28) | copy-start | bytes 12292
  165.7 20.5 %copy-start.1 = (f32[1,1024]{1,0:T(1,128)}, f32[1,1024]{1,0:T(1,128)S(1)}, u32[]{:S(2)}) copy-start(f32[1,1024]{1,0:T(1,128)S(1)} %get-tuple-element.29) | copy-start | bytes 12292
  165.8 20.5 %copy-start.2 = (f32[1,1024]{1,0:T(1,128)}, f32[1,1024]{1,0:T(1,128)S(1)}, u32[]{:S(2)}) copy-start(f32[1,1024]{1,0:T(1,128)S(1)} %get-tuple-element.30) | copy-start | bytes 12292

commit v3 on v2

--- a/solution.py
+++ b/solution.py
@@ -32,7 +32,7 @@
 
 
 def stack_kernel(n_model, n_data, chunk, batch_total,
-                 w_ref, u_ref, x_hbm, t_hbm,
+                 w0_ref, w1_ref, w2_ref, u0_ref, u1_ref, u2_ref, x_hbm, t_hbm,
                  dx_hbm, g_ref, small_ref,
                  dw_ref, pair, far_l, far_r, near_l, near_r, tiles, W, WT, U, T, xb, x1, x2, y0, y1, e2, e1, e0, dxb, sums,
                  u_send, u_recv, w_send, w_fwd, w_d2d, wl, wr, wf, wp,
@@ -40,7 +40,9 @@
                  x_sem, dx_loc, dx_send, dx_recv,
                  p_send, p_recv, fl, fr, f_send, nl, nr, n_send, gl, gr, gf, g_send, gf_send, s_send, s_recv):
     n_chips = n_model // CORES
-    n_layers, shard, width = w_ref.shape
+    w_refs = (w0_ref, w1_ref, w2_ref)
+    n_layers = len(w_refs)
+    shard, width = w0_ref.shape
     rows = x_hbm.shape[0] // CORES
     n_chunk = rows // chunk
     half = chunk // 2
@@ -62,6 +64,7 @@
         cp.start()
 
     my_data = lax.axis_index("data")
+    U[me] = jnp.concatenate([u0_ref[...], u1_ref[...], u2_ref[...], jnp.zeros((8 - n_layers, shard), F32)], axis=0)
 
     def cell(d, m):
         return {"data": d, "model": m}
@@ -80,8 +83,8 @@
 
     def send_w(k):
         for nb, rsem in ((right, wl), (left, wr)):
-            remote(w_ref.at[k], W.at[k, pl.ds(mrow, shard)], w_send.at[k], rsem.at[k], nb * CORES + core)
-        remote(w_ref.at[k], W.at[k, pl.ds(mrow, shard)], w_d2d.at[k], wp.at[k], partner)
+            remote(w_refs[k], W.at[k, pl.ds(mrow, shard)], w_send.at[k], rsem.at[k], nb * CORES + core)
+        remote(w_refs[k], W.at[k, pl.ds(mrow, shard)], w_d2d.at[k], wp.at[k], partner)
 
     def rows_of(c):
         return pl.multiple_of((c * CORES + core) * shard, shard)
@@ -129,15 +132,15 @@
 
     send_w(0)
     for step in range(1, n_model):
-        remote(u_ref, U.at[me], u_send, u_recv, (me + step) % n_model)
+        remote(U.at[me], U.at[me], u_send, u_recv, (me + step) % n_model)
     send_w(1)
     send_w(2)
     own_t = pltpu.make_async_copy(t_hbm.at[pl.ds(pl.multiple_of(row0, rows), rows)], T.at[me], t_own)
     own_t.start()
     load_x(0, 0).start()
-    U[me] = u_ref[...]
+    load_x(1, 1).start()
     for k in range(n_layers):
-        W[k, pl.ds(mrow, shard)] = w_ref[k]
+        W[k, pl.ds(mrow, shard)] = w_refs[k][...]
     sums[...] = jnp.zeros_like(sums)
     dw_ref[...] = jnp.zeros_like(dw_ref)
     tiles[my_data * CORES + core] = jnp.zeros((8, LANES), F32)
@@ -177,63 +180,86 @@
     inv = [1.0 / small_ref[2 * n_layers + k:2 * n_layers + k + 1, 0:1] for k in range(n_layers)]
     blocks = [slice(n * NBLK, (n + 1) * NBLK) for n in range(width // NBLK)]
     own_cols = pl.multiple_of(chip * CORES * shard, CORES * shard)
-
-    def add_sum(i, val):
-        sums[i] += jnp.sum(val.reshape(chunk // 8, 8, NBLK), axis=0)
-
-    def body(r, carry):
-        slot = r % 2
-        load_x(r, slot).wait()
-
-        @pl.when(r + 1 < n_chunk)
+    subs = [pl.ds(h * chunk, chunk) for h in range(2)]
+
+    def fold(val):
+        return jnp.sum(val.reshape(chunk // 8, 8, NBLK), axis=0)
+
+    def body(i, carry):
+        par = i % 2
+        base = pl.multiple_of(2 * par, 2)
+        for h in range(2):
+            load_x(2 * i + h, base + h).wait()
+
+        @pl.when(2 * i + 2 < n_chunk)
         def _():
-            load_x(r + 1, 1 - slot).start()
-
-        @pl.when(r + 2 < n_chunk)
+            for h in range(2):
+                load_x(2 * i + 2 + h, 2 - base + h).start()
+            send_t(2 * i + 2)
+
+        forward_t(2 * i + 1)
+        for blk in blocks:
+            for h, sub in enumerate(subs):
+                y_val = dot(xb[base + h], WT[0, :, blk]) * inv[0]
+                y0[sub, blk] = y_val
+                x1[sub, blk] = jnp.maximum(y_val, 0.2 * y_val).astype(BF16)
+        for h, sub in enumerate(subs):
+            for blk in blocks:
+                y_val = dot(x1[sub], WT[1, :, blk]) * inv[1]
+                y1[sub, blk] = y_val
+                x2[sub, blk] = jnp.maximum(y_val, 0.2 * y_val).astype(BF16)
+
+        @pl.when(2 * i + 2 < n_chunk)
         def _():
-            send_t(r + 2)
-
-        xin = xb.at[slot]
-        for src, k, yk, xk in ((xin, 0, y0, x1), (x1, 1, y1, x2)):
+            send_t(2 * i + 3)
+            forward_t(2 * i + 2)
+
+        for h in range(2):
+            wait_bytes(T.at[pl.ds(far * CORES, CORES), pl.ds((2 * i + h) * chunk, chunk)], tf.at[2 * i + h])
+            wait_bytes(T.at[partner, pl.ds((2 * i + h) * chunk, chunk)], tp.at[2 * i + h])
+
+        loss_sum = jnp.zeros((8, NBLK), F32)
+        c_sum = [jnp.zeros((8, NBLK), F32) for _ in range(n_layers)]
+        for h, sub in enumerate(subs):
+            trow = pl.ds(pl.multiple_of((2 * i + h) * chunk, chunk), chunk)
+            for n, blk in enumerate(blocks):
+                y_val = dot(x2[sub], WT[2, :, blk]) * inv[2]
+                t_val = jnp.concatenate([T[2 * n, trow], T[2 * n + 1, trow]], axis=1).astype(F32)
+                res = y_val - t_val
+                loss_sum += fold(res * res)
+                g_val = res * (1.0 / batch_total)
+                c_sum[2] += fold(g_val * y_val)
+                e2[sub, blk] = g_val.astype(BF16)
+
+        def back(k, h, ek, yk, store):
+            sub = subs[h]
             for blk in blocks:
-                y_val = dot(src[...], WT[k, :, blk]) * inv[k]
-                yk[:, blk] = y_val
-                xk[:, blk] = jnp.maximum(y_val, 0.2 * y_val).astype(BF16)
-
-        @pl.when(r + 1 < n_chunk)
-        def _():
-            forward_t(r + 1)
-
-        wait_bytes(T.at[pl.ds(far * CORES, CORES), pl.ds(r * chunk, chunk)], tf.at[r])
-        wait_bytes(T.at[partner, pl.ds(r * chunk, chunk)], tp.at[r])
-
-        @pl.when(r >= 2)
-        def _():
-            out_wait(r - 2, slot)
-
-        trow = pl.ds(pl.multiple_of(r * chunk, chunk), chunk)
-        for n, blk in enumerate(blocks):
-            y_val = dot(x2[...], WT[2, :, blk]) * inv[2]
-            t_val = jnp.concatenate([T[2 * n, trow], T[2 * n + 1, trow]], axis=1).astype(F32)
-            res = y_val - t_val
-            add_sum(3, res * res)
-            g_val = res / batch_total
-            add_sum(2, g_val * y_val)
-            e2[:, blk] = g_val.astype(BF16)
-        for k, ek, yk, en in ((2, e2, y1, e1), (1, e1, y0, e0)):
-            for blk in blocks:
-                r_val = (dot(ek[...], W[k, :, blk]) * inv[k]).astype(BF16).astype(F32)
-                y_val = yk[:, blk]
+                r_val = (dot(ek[sub], W[k, :, blk]) * inv[k]).astype(BF16).astype(F32)
+                y_val = yk[sub, blk]
                 g_val = jnp.where(y_val > 0, r_val, 0.2 * r_val)
-                add_sum(k - 1, g_val * y_val)
-                en[:, blk] = g_val.astype(BF16)
-        for blk in blocks:
-            dxb[slot, :, blk] = (dot(e0[...], W[0, :, blk]) * inv[0]).astype(BF16)
-        out_copy(r, slot).start()
-        out_remote(r, slot).start()
-        for k, ek, xk in ((2, e2, x2), (1, e1, x1), (0, e0, xin)):
-            e_own = ek[:, pl.ds(own_cols, CORES * shard)].T
-            dw_ref[k] += dot(e_own, xk[...])
+                c_sum[k - 1] += fold(g_val * y_val)
+                store(h, blk, g_val.astype(BF16))
+
+        def store_e1(h, blk, val):
+            e1[subs[h], blk] = val
+
+        def store_e0(h, blk, val):
+            e0[2 * i + h, :, blk] = val
+
+        def weight_grad(k, e_own, x_val):
+            dw_ref[k] += dot(e_own.T, x_val)
+
+        back(2, 0, e2, y1, store_e1)
+        back(2, 1, e2, y1, store_e1)
+        weight_grad(2, e2[:, pl.ds(own_cols, CORES * shard)], x2[...])
+        back(1, 0, e1, y0, store_e0)
+        back(1, 1, e1, y0, store_e0)
+        weight_grad(1, e1[:, pl.ds(own_cols, CORES * shard)], x1[...])
+        for h in range(2):
+            weight_grad(0, e0[2 * i + h, :, pl.ds(own_cols, CORES * shard)], xb[base + h])
+        for k in range(n_layers):
+            sums[k] += c_sum[k]
+        sums[n_layers] += loss_sum
         return carry
 
     def out_rows(r):
@@ -251,7 +277,22 @@
         out_copy(r, slot).wait()
         out_remote(r, slot).wait_send()
 
-    lax.fori_loop(0, n_chunk, body, 0)
+    lax.fori_loop(0, n_chunk // 2, body, 0)
+
+    pending = list(range(n_chunk))
+
+    def next_dx():
+        if not pending:
+            return
+        r = pending.pop(0)
+        slot = r % 2
+        if r >= 2:
+            out_wait(r - 2, slot)
+        for blk in blocks:
+            dxb[slot, :, blk] = (dot(e0[r], W[0, :, blk]) * inv[0]).astype(BF16)
+        out_copy(r, slot).start()
+        out_remote(r, slot).start()
+
 
     for i in range(4):
         tot = jnp.sum(jnp.sum(sums[i], axis=0, keepdims=True), axis=1, keepdims=True)
@@ -283,6 +324,7 @@
     remote_to(mine, mine, s_send, s_recv, dev(partner))
     for step, c in column:
         remote_to(mine, mine, s_send, s_recv, cell((my_data + step) % n_data, chip * CORES + c))
+    next_dx()
     for k in order:
         wait_bytes(pair.at[k], p_recv.at[k])
         dw_ref[k, pl.ds(mine_rows, shard)] += pair[k]
@@ -290,7 +332,9 @@
         remote_to(dw_ref.at[k, acc_quarter(opp, hrows, hrows)], far_r.at[k], f_send.at[k], fr.at[k], to_down)
         remote_to(dw_ref.at[k, acc_quarter(up, hrows, hrows)], near_l.at[k, pl.ds(hrows, hrows)], n_send.at[k], nl.at[k], to_up)
         remote_to(dw_ref.at[k, acc_quarter(down, 0, hrows)], near_r.at[k, pl.ds(0, hrows)], n_send.at[k], nr.at[k], to_down)
-    for k in order:
+    next_dx()
+    for k in order:
+        next_dx()
         wait_bytes(far_l.at[k], fl.at[k])
         dw_ref[k, acc_quarter(up, 0, hrows)] += far_l[k]
         remote_to(dw_ref.at[k, acc_quarter(up, 0, hrows)], near_l.at[k, pl.ds(0, hrows)], n_send.at[k], nl.at[k], to_up)
@@ -298,6 +342,7 @@
         dw_ref[k, acc_quarter(down, hrows, hrows)] += far_r[k]
         remote_to(dw_ref.at[k, acc_quarter(down, hrows, hrows)], near_r.at[k, pl.ds(hrows, hrows)], n_send.at[k], nr.at[k], to_down)
     for k in order:
+        next_dx()
         wait_bytes(near_l.at[k], nl.at[k])
         wait_bytes(near_r.at[k], nr.at[k])
         g_ref[k, quarter(my_data, 0, qrows)] = dw_ref[k, acc_quarter(my_data, 0, qrows)] + near_l[k] + near_r[k]
@@ -312,6 +357,8 @@
         ref = g_ref.at[k, quarter(up, hrows, hrows)]
         remote_to(ref, ref, gf_send.at[k], gf.at[k], to_down)
 
+    while pending:
+        next_dx()
     out_wait(n_chunk - 2, 0)
     out_wait(n_chunk - 1, 1)
 
@@ -335,6 +382,36 @@
         wait_bytes(pair.at[k, pl.ds(0, 2 * qrows)], n_send.at[k])
         wait_bytes(pair.at[k, pl.ds(0, 2 * qrows)], g_send.at[k])
         wait_bytes(near_l.at[k], gf_send.at[k])
+
+
+def finish_kernel(batch_total, dx_in, g_ref, small_ref, dx_out, loss_ref, dw0, dw1, dw2,
+                  un0, un1, un2, v0, v1, v2, sig_ref, buf, in_sem, out_sem):
+    n_layers, shard, width = g_ref.shape
+    slots, rows, _ = buf.shape
+    me = lax.axis_index("model")
+    loads = [pltpu.make_async_copy(dx_in.at[pl.ds(n * rows, rows)], buf.at[n], in_sem.at[n]) for n in range(slots)]
+    stores = [pltpu.make_async_copy(buf.at[n], dx_out.at[pl.ds(n * rows, rows)], out_sem.at[n]) for n in range(slots)]
+    for load in loads:
+        load.start()
+    mine = pl.ds(pl.multiple_of(me * shard, shard), shard)
+    sigs = []
+    for k, (dw, un, v) in enumerate(((dw0, un0, v0), (dw1, un1, v1), (dw2, un2, v2))):
+        v_row = small_ref[k:k + 1]
+        u_row = small_ref[n_layers + k:n_layers + k + 1, mine]
+        sigma = small_ref[2 * n_layers + k:2 * n_layers + k + 1, 0:1]
+        scale = small_ref[3 * n_layers + k:3 * n_layers + k + 1, 0:1] / sigma
+        u_col = jnp.broadcast_to(u_row, (8, shard)).T[:, 0:1]
+        dw[...] = g_ref[k] * (1.0 / sigma) - (scale * u_col) * v_row
+        un[...] = u_row
+        v[...] = v_row
+        sigs.append(sigma)
+    sig_ref[...] = jnp.concatenate(sigs, axis=1)
+    loss_ref[...] = (0.5 / batch_total) * small_ref[4 * n_layers:4 * n_layers + 1, 0:1]
+    for load, store in zip(loads, stores):
+        load.wait()
+        store.start()
+    for store in stores:
+        store.wait()
 
 
 def solution(mesh):
@@ -353,8 +430,6 @@
         rows = rows_all // CORES
         chunk = rows // 8
         n_chunk = rows // chunk
-        w_all = jnp.stack([w_in, w_mid, w_out])
-        u_all = jnp.concatenate([jnp.stack([u_in, u_mid, u_out]), jnp.zeros((5, shard), F32)], axis=0)
         vm = pltpu.VMEM
         dma = pltpu.SemaphoreType.DMA
         any_spec = pl.BlockSpec(memory_space=pl.ANY)
@@ -364,7 +439,7 @@
             out_shape=(jax.ShapeDtypeStruct((rows_all, width), BF16),
                        jax.ShapeDtypeStruct((3, shard, width), F32),
                        jax.ShapeDtypeStruct((16, width), F32)),
-            in_specs=[vmem_spec, vmem_spec, any_spec, any_spec],
+            in_specs=[vmem_spec] * 6 + [any_spec, any_spec],
             out_specs=(any_spec, vmem_spec, vmem_spec),
             scratch_shapes=[
                 vm((3, CORES * shard, width), F32), vm((3, shard, width), F32),
@@ -373,27 +448,29 @@
                 vm((data_size * CORES, 8, LANES), F32),
                 vm((3, width, width), BF16), vm((3, width, width), BF16),
                 vm((n_model, 8, shard), F32), vm((n_model, rows, shard), BF16),
-                vm((2, chunk, width), BF16), vm((chunk, width), BF16), vm((chunk, width), BF16),
-                vm((chunk, width), F32), vm((chunk, width), F32),
-                vm((chunk, width), BF16), vm((chunk, width), BF16), vm((chunk, width), BF16),
+                vm((4, chunk, width), BF16), vm((2 * chunk, width), BF16), vm((2 * chunk, width), BF16),
+                vm((2 * chunk, width), F32), vm((2 * chunk, width), F32),
+                vm((2 * chunk, width), BF16), vm((2 * chunk, width), BF16), vm((n_chunk, chunk, width), BF16),
                 vm((2, chunk, width), BF16), vm((4, 8, NBLK), F32),
                 dma, dma, dma((3,)), dma((3,)), dma((3,)), dma((3,)), dma((3,)), dma((3,)), dma((3,)),
                 dma, dma((n_chunk,)), dma((n_chunk,)), dma((n_chunk,)), dma((n_chunk,)), dma((n_chunk,)), dma((n_chunk,)),
-                dma((2,)), dma((2,)), dma((2,)), dma((n_chunk,)),
+                dma((4,)), dma((2,)), dma((2,)), dma((n_chunk,)),
                 *[dma((3,)) for _ in range(13)], dma, dma],
             compiler_params=pltpu.CompilerParams(collective_id=0, has_side_effects=True,
-                                                 vmem_limit_bytes=60 * 1024 * 1024),
-        )(w_all, u_all, x_in, target)
-
-        me = lax.axis_index("model")
-        v_rows = small[0:3]
-        sigma = small[6:9, 0]
-        scal = small[9:13, 0]
-        u_next = lax.dynamic_slice_in_dim(small[3:6], me * shard, shard, axis=1)
-        dws = [g_mat[k] / sigma[k] - (scal[k] / sigma[k]) * (u_next[k][:, None] * v_rows[k][None, :]) for k in range(3)]
-        loss_val = 0.5 / batch_total * scal[3]
-        return (loss_val.reshape(1), dx, dws[0], dws[1], dws[2],
-                u_next[0], u_next[1], u_next[2], v_rows[0], v_rows[1], v_rows[2], sigma)
+                                                 vmem_limit_bytes=67043328),
+        )(w_in, w_mid, w_out, u_in.reshape(1, shard), u_mid.reshape(1, shard), u_out.reshape(1, shard), x_in, target)
+
+        slots = 16
+        sds = jax.ShapeDtypeStruct
+        outs = pl.pallas_call(
+            functools.partial(finish_kernel, batch_total),
+            out_shape=([sds((rows_all, width), BF16), sds((1, 1), F32)] + [sds((shard, width), F32)] * 3
+                       + [sds((1, shard), F32)] * 3 + [sds((1, width), F32)] * 3 + [sds((1, 3), F32)]),
+            in_specs=[any_spec, vmem_spec, vmem_spec],
+            out_specs=[any_spec] + [vmem_spec] * 11,
+            scratch_shapes=[vm((slots, rows_all // slots, width), BF16), dma((slots,)), dma((slots,))],
+        )(dx, g_mat, small)
+        return (outs[1].reshape(1), outs[0], outs[2], outs[3], outs[4]) + tuple(o.reshape(-1) for o in outs[5:])
 
     in_specs = (batch_spec, row_spec, row_spec, row_spec, vec_spec, vec_spec, vec_spec, target_spec)
     out_specs = (part_spec, batch_spec, row_spec, row_spec, row_spec, vec_spec, vec_spec, vec_spec, part_spec, part_spec, part_spec, part_spec)

time: 188 us -> 179 us (0.952)
  Pallas kernels: 154 us -> 178 us
  local copies, waits for them, and re-layouts: 18.4 us -> 0 us
  other arithmetic: 8.02 us -> 0 us
  between operations: 6.5 us -> 0.84 us
    pallas_call x0 -> x1, Pallas kernels: none -> 14.7 us  [local_step(): pl.pallas_call(functools.partial(finish_kernel, batch_total), out_shape=[...]
    unnamed x13 -> x0, local copies, waits for them, and re-layouts: 13.9 us -> none
    pallas_call x1, Pallas kernels: 154 us -> 164 us  [local_step(): pl.pallas_call(functools.partial(stack_kernel, n_model, data_size, chunk,...]
    sub x1 -> x0, other arithmetic: 4.6 us -> none  [local_step(): g_mat[k] / sigma[k]]
    slice x4 -> x0, local copies, waits for them, and re-layouts: 4.38 us -> none  [the longest x1 1.41 us: local_step(): sigma[k]]
    another operation x1 -> x0, other arithmetic: 2.08 us -> none  [local_step(): w_all = jnp.stack([w_in, w_mid, w_out])]
where the time goes in v3:
time: 179 us
  Pallas kernels  178 us (99%)
    pallas_call x1, Pallas kernels, local_step(): pl.pallas_call(functools.partial(stack_kernel, n_model, data_size, chunk,...  164 us
    pallas_call x1, Pallas kernels, local_step(): pl.pallas_call(functools.partial(finish_kernel, batch_total), out_shape=[...  14.7 us

profile of v3, /device:TPU:97, one launch (start us, length us, event | category | flops | bytes accessed | tf_op | source)
XLA Modules:
  0.0 179.3 jit_solution(7943775603833768357)
XLA Ops:
  0.6 163.8 %shard_map.175 = (bf16[8192,1024]{1,0:T(8,128)(2,1)}, f32[3,128,1024]{2,1,0:T(8,128)}, f32[16,1024]{1,0:T(8,128)}) custom-call(bf16[128,1024]{1,0:T(8,128)(2,1)} %w0_ref.1, bf16[128,1024]{1,0:T(8,128)(2,1)} %w1_ref.1, bf16[128,1024]{1,0:T(8,128)(2,1)} %w2_ref.1, f32[1,128]{1,0:T(1,128)} %bitcast.11, f32[1,128]{1,0:T(1,128)} %bitcast.12, f32[1,128]{1,0:T(1,128)} %bitcast.13, ...), custom_call_target="tpu_custom_call" | custom-call | tf_op jit(solution)/shard_map/pallas_call | solution.py:437
  164.5 14.7 %shard_map.176 = (bf16[8192,1024]{1,0:T(8,128)(2,1)}, f32[1,1]{1,0:T(1,128)}, f32[128,1024]{1,0:T(8,128)}, f32[128,1024]{1,0:T(8,128)}, f32[128,1024]{1,0:T(8,12...) custom-call(bf16[8192,1024]{1,0:T(8,128)(2,1)} %get-tuple-element.27, ...), custom_call_target="tpu_custom_call" | custom-call | tf_op jit(solution)/shard_map/pallas_call | solution.py:465

commit v4 on v3

--- a/solution.py
+++ b/solution.py
@@ -35,7 +35,7 @@
                  w0_ref, w1_ref, w2_ref, u0_ref, u1_ref, u2_ref, x_hbm, t_hbm,
                  dx_hbm, g_ref, small_ref,
                  dw_ref, pair, far_l, far_r, near_l, near_r, tiles, W, WT, U, T, xb, x1, x2, y0, y1, e2, e1, e0, dxb, sums,
-                 u_send, u_recv, w_send, w_fwd, w_d2d, wl, wr, wf, wp,
+                 u_send, u_recv, w_send, w_fwd, w_d2d, wl, wr, wf, wp, wy_send, wy_up, wy_down, wy_far,
                  t_own, t_send, t_fwd, tl, tr, tf, tp,
                  x_sem, dx_loc, dx_send, dx_recv,
                  p_send, p_recv, fl, fr, f_send, nl, nr, n_send, gl, gr, gf, g_send, gf_send, s_send, s_recv):
@@ -107,6 +107,50 @@
         remote(src_f, src_f, w_d2d.at[k], wp.at[k], partner)
         wait_bytes(W.at[k, pl.ds(0, n_chips * shard)], wp.at[k])
 
+    qrows = shard // n_data
+    hrows = qrows // 2
+    up = (my_data + 1) % n_data
+    down = (my_data + n_data - 1) % n_data
+    opp = (my_data + 2) % n_data
+    to_up, to_down = {"data": up}, {"data": down}
+
+    def w_part(k, c, d, off, n):
+        return W.at[k, pl.ds(pl.multiple_of((c * CORES + core) * shard + d * qrows + off, hrows), n)]
+
+    def remote_to(src, dst, ssem, rsem, device):
+        pltpu.make_async_remote_copy(src_ref=src, dst_ref=dst, send_sem=ssem, recv_sem=rsem,
+                                     device_id=device, device_id_type=MESH_ID).start()
+
+    def send_wq(k):
+        src = w_refs[k].at[pl.ds(pl.multiple_of(my_data * qrows, qrows), qrows)]
+        for nb, rsem in ((right, wl), (left, wr), (far, wf)):
+            remote(src, w_part(k, chip, my_data, 0, qrows), w_send.at[k], rsem.at[k], nb * CORES + core)
+        remote(w_refs[k], W.at[k, pl.ds(mrow, shard)], w_d2d.at[k], wp.at[k], partner)
+
+    def spread_wq(k):
+        for c, rsem in ((left, wl), (right, wr), (far, wf)):
+            ref = w_part(k, c, my_data, 0, qrows)
+            wait_bytes(ref, rsem.at[k])
+            remote_to(ref, ref, wy_send.at[k], wy_down.at[k], to_up)
+            remote_to(ref, ref, wy_send.at[k], wy_up.at[k], to_down)
+
+    def relay_wq(k):
+        wait_bytes(W.at[k, pl.ds(0, 3 * qrows)], wy_down.at[k])
+        for c in (left, right, far):
+            ref = w_part(k, c, down, 0, hrows)
+            remote_to(ref, ref, w_fwd.at[k], wy_far.at[k], to_up)
+        wait_bytes(W.at[k, pl.ds(0, 3 * qrows)], wy_up.at[k])
+        for c in (left, right, far):
+            ref = w_part(k, c, up, hrows, hrows)
+            remote_to(ref, ref, w_fwd.at[k], wy_far.at[k], to_down)
+
+    def finish_wq(k):
+        wait_bytes(W.at[k, pl.ds(0, 3 * qrows)], wy_far.at[k])
+        for c in (left, right, far):
+            ref = W.at[k, pl.ds(rows_of(c), shard)]
+            remote(ref, ref, w_d2d.at[k], wp.at[k], partner)
+        wait_bytes(W.at[k, pl.ds(0, n_chips * shard)], wp.at[k])
+
     def send_t(r):
         for c in range(CORES):
             src = t_hbm.at[pl.ds(c * rows + r * chunk, chunk)]
@@ -130,11 +174,12 @@
         return pltpu.make_async_copy(x_hbm.at[pl.ds(pl.multiple_of(row0 + r * chunk, chunk), chunk)],
                                      xb.at[slot], x_sem.at[slot])
 
+    send_wq(1)
+    send_wq(2)
     send_w(0)
     for step in range(1, n_model):
         remote(U.at[me], U.at[me], u_send, u_recv, (me + step) % n_model)
-    send_w(1)
-    send_w(2)
+    send_t(0)
     own_t = pltpu.make_async_copy(t_hbm.at[pl.ds(pl.multiple_of(row0, rows), rows)], T.at[me], t_own)
     own_t.start()
     load_x(0, 0).start()
@@ -145,17 +190,20 @@
     dw_ref[...] = jnp.zeros_like(dw_ref)
     tiles[my_data * CORES + core] = jnp.zeros((8, LANES), F32)
     small_ref[...] = jnp.zeros_like(small_ref)
+    spread_wq(1)
+    spread_wq(2)
     wait_bytes(U.at[pl.ds(0, n_model - 1)], u_recv)
     wait_bytes(U.at[pl.ds(0, n_model - 1)], u_send)
-
     forward_w(0)
+    send_t(1)
+    relay_wq(1)
     for k in range(n_layers):
-        if k + 1 < n_layers:
-            forward_w(k + 1)
+        if k == 0:
+            finish_w(0)
         else:
-            send_t(0)
-            send_t(1)
-        finish_w(k)
+            if k == 2:
+                send_t(2)
+            finish_wq(k)
         for i in range(width // NBLK):
             for j in range(width // NBLK):
                 blk = W[k, i * NBLK:(i + 1) * NBLK, j * NBLK:(j + 1) * NBLK]
@@ -171,12 +219,15 @@
         small_ref[k:k + 1] = v_row
         small_ref[n_layers + k:n_layers + k + 1] = s_row / sigma
         small_ref[2 * n_layers + k:2 * n_layers + k + 1] = jnp.broadcast_to(sigma, (1, width))
+        if k == 0:
+            relay_wq(2)
     for k in range(n_layers):
-        wait_bytes(W.at[k, pl.ds(0, CORES * shard)], w_send.at[k])
-        wait_bytes(W.at[k, pl.ds(0, shard)], w_fwd.at[k])
+        wait_bytes(W.at[k, pl.ds(0, 3 * qrows if k else CORES * shard)], w_send.at[k])
+        wait_bytes(W.at[k, pl.ds(0, 6 * hrows if k else shard)], w_fwd.at[k])
+        if k:
+            wait_bytes(W.at[k, pl.ds(0, 6 * qrows)], wy_send.at[k])
         wait_bytes(W.at[k, pl.ds(0, n_chips * shard)], w_d2d.at[k])
     own_t.wait()
-    forward_t(0)
     inv = [1.0 / small_ref[2 * n_layers + k:2 * n_layers + k + 1, 0:1] for k in range(n_layers)]
     blocks = [slice(n * NBLK, (n + 1) * NBLK) for n in range(width // NBLK)]
     own_cols = pl.multiple_of(chip * CORES * shard, CORES * shard)
@@ -191,13 +242,19 @@
         for h in range(2):
             load_x(2 * i + h, base + h).wait()
 
+        forward_t(2 * i)
+        forward_t(2 * i + 1)
+
         @pl.when(2 * i + 2 < n_chunk)
         def _():
             for h in range(2):
                 load_x(2 * i + 2 + h, 2 - base + h).start()
-            send_t(2 * i + 2)
-
-        forward_t(2 * i + 1)
+            send_t(2 * i + 3)
+
+        @pl.when(2 * i + 4 < n_chunk)
+        def _():
+            send_t(2 * i + 4)
+
         for blk in blocks:
             for h, sub in enumerate(subs):
                 y_val = dot(xb[base + h], WT[0, :, blk]) * inv[0]
@@ -209,18 +266,11 @@
                 y1[sub, blk] = y_val
                 x2[sub, blk] = jnp.maximum(y_val, 0.2 * y_val).astype(BF16)
 
-        @pl.when(2 * i + 2 < n_chunk)
-        def _():
-            send_t(2 * i + 3)
-            forward_t(2 * i + 2)
-
-        for h in range(2):
-            wait_bytes(T.at[pl.ds(far * CORES, CORES), pl.ds((2 * i + h) * chunk, chunk)], tf.at[2 * i + h])
-            wait_bytes(T.at[partner, pl.ds((2 * i + h) * chunk, chunk)], tp.at[2 * i + h])
-
         loss_sum = jnp.zeros((8, NBLK), F32)
         c_sum = [jnp.zeros((8, NBLK), F32) for _ in range(n_layers)]
         for h, sub in enumerate(subs):
+            wait_bytes(T.at[pl.ds(far * CORES, CORES), pl.ds((2 * i + h) * chunk, chunk)], tf.at[2 * i + h])
+            wait_bytes(T.at[partner, pl.ds((2 * i + h) * chunk, chunk)], tp.at[2 * i + h])
             trow = pl.ds(pl.multiple_of((2 * i + h) * chunk, chunk), chunk)
             for n, blk in enumerate(blocks):
                 y_val = dot(x2[sub], WT[2, :, blk]) * inv[2]
@@ -299,20 +349,9 @@
         tiles[my_data * CORES + core, i:i + 1] = jnp.broadcast_to(tot, (1, LANES))
     mine = tiles.at[my_data * CORES + core]
 
-    def remote_to(src, dst, ssem, rsem, device):
-        pltpu.make_async_remote_copy(src_ref=src, dst_ref=dst, send_sem=ssem, recv_sem=rsem,
-                                     device_id=device, device_id_type=MESH_ID).start()
-
     order = (2, 1, 0)
     mine_rows = pl.multiple_of(core * shard, shard)
     other_rows = pl.multiple_of((1 - core) * shard, shard)
-    qrows = shard // n_data
-    hrows = qrows // 2
-    up = (my_data + 1) % n_data
-    down = (my_data + n_data - 1) % n_data
-    opp = (my_data + 2) % n_data
-    to_up, to_down = {"data": up}, {"data": down}
-
     def quarter(d, off, n):
         return pl.ds(pl.multiple_of(d * qrows + off, 8), n)
 
@@ -384,34 +423,45 @@
         wait_bytes(near_l.at[k], gf_send.at[k])
 
 
-def finish_kernel(batch_total, dx_in, g_ref, small_ref, dx_out, loss_ref, dw0, dw1, dw2,
-                  un0, un1, un2, v0, v1, v2, sig_ref, buf, in_sem, out_sem):
-    n_layers, shard, width = g_ref.shape
+def finish_kernel(batch_total, dx_in, g_hbm, small_ref, dx_out, loss_ref, dw0, dw1, dw2,
+                  un0, un1, un2, v0, v1, v2, sig_ref, buf, g_buf, d_buf, in_sem, out_sem, g_in, d_out):
+    n_layers, shard, width = g_buf.shape
     slots, rows, _ = buf.shape
     me = lax.axis_index("model")
     loads = [pltpu.make_async_copy(dx_in.at[pl.ds(n * rows, rows)], buf.at[n], in_sem.at[n]) for n in range(slots)]
     stores = [pltpu.make_async_copy(buf.at[n], dx_out.at[pl.ds(n * rows, rows)], out_sem.at[n]) for n in range(slots)]
-    for load in loads:
+    g_load = pltpu.make_async_copy(g_hbm, g_buf, g_in)
+    for load in loads[:slots // 2]:
         load.start()
+    g_load.start()
+    for load in loads[slots // 2:]:
+        load.start()
+    for load, store in zip(loads[:slots // 2], stores):
+        load.wait()
+        store.start()
+    g_load.wait()
     mine = pl.ds(pl.multiple_of(me * shard, shard), shard)
-    sigs = []
+    sigs, writes = [], []
     for k, (dw, un, v) in enumerate(((dw0, un0, v0), (dw1, un1, v1), (dw2, un2, v2))):
         v_row = small_ref[k:k + 1]
         u_row = small_ref[n_layers + k:n_layers + k + 1, mine]
         sigma = small_ref[2 * n_layers + k:2 * n_layers + k + 1, 0:1]
         scale = small_ref[3 * n_layers + k:3 * n_layers + k + 1, 0:1] / sigma
         u_col = jnp.broadcast_to(u_row, (8, shard)).T[:, 0:1]
-        dw[...] = g_ref[k] * (1.0 / sigma) - (scale * u_col) * v_row
+        d_buf[k] = g_buf[k] * (1.0 / sigma) - (scale * u_col) * v_row
+        writes.append(pltpu.make_async_copy(d_buf.at[k], dw, d_out.at[k]))
         un[...] = u_row
         v[...] = v_row
         sigs.append(sigma)
     sig_ref[...] = jnp.concatenate(sigs, axis=1)
     loss_ref[...] = (0.5 / batch_total) * small_ref[4 * n_layers:4 * n_layers + 1, 0:1]
-    for load, store in zip(loads, stores):
+    for load, store in zip(loads[slots // 2:], stores[slots // 2:]):
         load.wait()
         store.start()
-    for store in stores:
-        store.wait()
+    for write in writes:
+        write.start()
+    for copy in stores + writes:
+        copy.wait()
 
 
 def solution(mesh):
@@ -452,7 +502,7 @@
                 vm((2 * chunk, width), F32), vm((2 * chunk, width), F32),
                 vm((2 * chunk, width), BF16), vm((2 * chunk, width), BF16), vm((n_chunk, chunk, width), BF16),
                 vm((2, chunk, width), BF16), vm((4, 8, NBLK), F32),
-                dma, dma, dma((3,)), dma((3,)), dma((3,)), dma((3,)), dma((3,)), dma((3,)), dma((3,)),
+                dma, dma, *[dma((3,)) for _ in range(11)],
                 dma, dma((n_chunk,)), dma((n_chunk,)), dma((n_chunk,)), dma((n_chunk,)), dma((n_chunk,)), dma((n_chunk,)),
                 dma((4,)), dma((2,)), dma((2,)), dma((n_chunk,)),
                 *[dma((3,)) for _ in range(13)], dma, dma],
@@ -466,9 +516,10 @@
             functools.partial(finish_kernel, batch_total),
             out_shape=([sds((rows_all, width), BF16), sds((1, 1), F32)] + [sds((shard, width), F32)] * 3
                        + [sds((1, shard), F32)] * 3 + [sds((1, width), F32)] * 3 + [sds((1, 3), F32)]),
-            in_specs=[any_spec, vmem_spec, vmem_spec],
-            out_specs=[any_spec] + [vmem_spec] * 11,
-            scratch_shapes=[vm((slots, rows_all // slots, width), BF16), dma((slots,)), dma((slots,))],
+            in_specs=[any_spec, any_spec, vmem_spec],
+            out_specs=[any_spec, vmem_spec] + [any_spec] * 3 + [vmem_spec] * 7,
+            scratch_shapes=[vm((slots, rows_all // slots, width), BF16), vm((3, shard, width), F32), vm((3, shard, width), F32),
+                            dma((slots,)), dma((slots,)), dma, dma((3,))],
         )(dx, g_mat, small)
         return (outs[1].reshape(1), outs[0], outs[2], outs[3], outs[4]) + tuple(o.reshape(-1) for o in outs[5:])
 

time: 179 us -> 157 us (0.88)
  Pallas kernels: 178 us -> 156 us
    pallas_call x1, Pallas kernels: 164 us -> 142 us  [local_step(): pl.pallas_call(functools.partial(stack_kernel, n_model, data_size, chunk,...]
where the time goes in v4:
time: 157 us
  Pallas kernels  156 us (99%)
    pallas_call x1, Pallas kernels, local_step(): pl.pallas_call(functools.partial(stack_kernel, n_model, data_size, chunk,...  142 us
    pallas_call x1, Pallas kernels, local_step(): pl.pallas_call(functools.partial(finish_kernel, batch_total), out_shape=[...  14.9 us

profile of v4, /device:TPU:97, one launch (start us, length us, event | category | flops | bytes accessed | tf_op | source)
XLA Modules:
  0.0 157.3 jit_solution(14178559478996199851)
XLA Ops:
  0.6 141.6 %shard_map.175 = (bf16[8192,1024]{1,0:T(8,128)(2,1)}, f32[3,128,1024]{2,1,0:T(8,128)}, f32[16,1024]{1,0:T(8,128)}) custom-call(bf16[128,1024]{1,0:T(8,128)(2,1)} %w0_ref.1, bf16[128,1024]{1,0:T(8,128)(2,1)} %w1_ref.1, bf16[128,1024]{1,0:T(8,128)(2,1)} %w2_ref.1, f32[1,128]{1,0:T(1,128)} %bitcast.11, f32[1,128]{1,0:T(1,128)} %bitcast.12, f32[1,128]{1,0:T(1,128)} %bitcast.13, ...), custom_call_target="tpu_custom_call" | custom-call | tf_op jit(solution)/shard_map/pallas_call | solution.py:487
  142.2 14.9 %shard_map.176 = (bf16[8192,1024]{1,0:T(8,128)(2,1)}, f32[1,1]{1,0:T(1,128)}, f32[128,1024]{1,0:T(8,128)}, f32[128,1024]{1,0:T(8,128)}, f32[128,1024]{1,0:T(8,12...) custom-call(bf16[8192,1024]{1,0:T(8,128)(2,1)} %get-tuple-element.27, ...), custom_call_target="tpu_custom_call" | custom-call | tf_op jit(solution)/shard_map/pallas_call | solution.py:515

commit v5 on v4

--- a/solution.py
+++ b/solution.py
@@ -201,8 +201,6 @@
         if k == 0:
             finish_w(0)
         else:
-            if k == 2:
-                send_t(2)
             finish_wq(k)
         for i in range(width // NBLK):
             for j in range(width // NBLK):
@@ -249,22 +247,18 @@
         def _():
             for h in range(2):
                 load_x(2 * i + 2 + h, 2 - base + h).start()
+            send_t(2 * i + 2)
             send_t(2 * i + 3)
 
-        @pl.when(2 * i + 4 < n_chunk)
-        def _():
-            send_t(2 * i + 4)
-
+        xin = xb[pl.ds(base, 2)].reshape(2 * chunk, width)
         for blk in blocks:
-            for h, sub in enumerate(subs):
-                y_val = dot(xb[base + h], WT[0, :, blk]) * inv[0]
-                y0[sub, blk] = y_val
-                x1[sub, blk] = jnp.maximum(y_val, 0.2 * y_val).astype(BF16)
-        for h, sub in enumerate(subs):
-            for blk in blocks:
-                y_val = dot(x1[sub], WT[1, :, blk]) * inv[1]
-                y1[sub, blk] = y_val
-                x2[sub, blk] = jnp.maximum(y_val, 0.2 * y_val).astype(BF16)
+            y_val = dot(xin, WT[0, :, blk]) * inv[0]
+            y0[:, blk] = y_val
+            x1[:, blk] = jnp.maximum(y_val, 0.2 * y_val).astype(BF16)
+        for blk in blocks:
+            y_val = dot(x1[...], WT[1, :, blk]) * inv[1]
+            y1[:, blk] = y_val
+            x2[:, blk] = jnp.maximum(y_val, 0.2 * y_val).astype(BF16)
 
         loss_sum = jnp.zeros((8, NBLK), F32)
         c_sum = [jnp.zeros((8, NBLK), F32) for _ in range(n_layers)]
@@ -431,14 +425,9 @@
     loads = [pltpu.make_async_copy(dx_in.at[pl.ds(n * rows, rows)], buf.at[n], in_sem.at[n]) for n in range(slots)]
     stores = [pltpu.make_async_copy(buf.at[n], dx_out.at[pl.ds(n * rows, rows)], out_sem.at[n]) for n in range(slots)]
     g_load = pltpu.make_async_copy(g_hbm, g_buf, g_in)
-    for load in loads[:slots // 2]:
+    g_load.start()
+    for load in loads:
         load.start()
-    g_load.start()
-    for load in loads[slots // 2:]:
-        load.start()
-    for load, store in zip(loads[:slots // 2], stores):
-        load.wait()
-        store.start()
     g_load.wait()
     mine = pl.ds(pl.multiple_of(me * shard, shard), shard)
     sigs, writes = [], []
@@ -455,11 +444,11 @@
         sigs.append(sigma)
     sig_ref[...] = jnp.concatenate(sigs, axis=1)
     loss_ref[...] = (0.5 / batch_total) * small_ref[4 * n_layers:4 * n_layers + 1, 0:1]
-    for load, store in zip(loads[slots // 2:], stores[slots // 2:]):
+    for write in writes:
+        write.start()
+    for load, store in zip(loads, stores):
         load.wait()
         store.start()
-    for write in writes:
-        write.start()
     for copy in stores + writes:
         copy.wait()
 
@@ -510,7 +499,7 @@
                                                  vmem_limit_bytes=67043328),
         )(w_in, w_mid, w_out, u_in.reshape(1, shard), u_mid.reshape(1, shard), u_out.reshape(1, shard), x_in, target)
 
-        slots = 16
+        slots = 32
         sds = jax.ShapeDtypeStruct
         outs = pl.pallas_call(
             functools.partial(finish_kernel, batch_total),

time: 157 us -> 156 us (level)
  no operation moved by 1% of the time
where the time goes in v5:
time: 156 us
  Pallas kernels  155 us (99%)
    pallas_call x1, Pallas kernels, local_step(): pl.pallas_call(functools.partial(stack_kernel, n_model, data_size, chunk,...  140 us
    pallas_call x1, Pallas kernels, local_step(): pl.pallas_call(functools.partial(finish_kernel, batch_total), out_shape=[...  14.8 us

profile of v5, /device:TPU:97, one launch (start us, length us, event | category | flops | bytes accessed | tf_op | source)
XLA Modules:
  0.0 156.1 jit_solution(9674351846953757726)
XLA Ops:
  0.6 140.5 %shard_map.175 = (bf16[8192,1024]{1,0:T(8,128)(2,1)}, f32[3,128,1024]{2,1,0:T(8,128)}, f32[16,1024]{1,0:T(8,128)}) custom-call(bf16[128,1024]{1,0:T(8,128)(2,1)} %w0_ref.1, bf16[128,1024]{1,0:T(8,128)(2,1)} %w1_ref.1, bf16[128,1024]{1,0:T(8,128)(2,1)} %w2_ref.1, f32[1,128]{1,0:T(1,128)} %bitcast.11, f32[1,128]{1,0:T(1,128)} %bitcast.12, f32[1,128]{1,0:T(1,128)} %bitcast.13, ...), custom_call_target="tpu_custom_call" | custom-call | tf_op jit(solution)/shard_map/pallas_call | solution.py:476
  141.1 14.8 %shard_map.176 = (bf16[8192,1024]{1,0:T(8,128)(2,1)}, f32[1,1]{1,0:T(1,128)}, f32[128,1024]{1,0:T(8,128)}, f32[128,1024]{1,0:T(8,128)}, f32[128,1024]{1,0:T(8,12...) custom-call(bf16[8192,1024]{1,0:T(8,128)(2,1)} %get-tuple-element.27, ...), custom_call_target="tpu_custom_call" | custom-call | tf_op jit(solution)/shard_map/pallas_call | solution.py:504
